TPU v7x, 32 devices: a whole 2x2x4 slice. The times are simulated.
32 devices in a mesh: gx: 4 (over y, x), gy: 2 (over core), gz: 4 (over z).
Axes of the slice: x: 2, y: 2, z: 4, core: 2. Of those that a mesh axis runs over, the one named last changes fastest.
Arguments:
- populations: float32 [2, 19, 16, 32, 512], P(None, None, 'gx', 'gy', 'gz'), may hold values from 0.01 to 0.2
- solid: int32 [16, 32, 512], P('gx', 'gy', 'gz'), may hold values 0 or 1
Outputs:
- read: float32 [2, 19, 16, 32, 512], P(None, None, 'gx', 'gy', 'gz')
All inputs are finite; a program needn't handle non-finite values. No bound on the sum of `solid` on one device may be relied on, other than what follows from the above.
Results may differ from a plain program's by a relative error of at most 0.0001.
Values sent between devices are 32-bit elements; how exact they have to be, the bound alone decides.
No kernel may reach another device: no remote copies, remote signals or barrier semaphores. Data moves between devices by JAX's collectives and lax.ppermute only.
A program may use at most 64 MiB of HBM per device.

v0:
```python
import jax
import jax.numpy as jnp
import numpy as np
from jax import lax
from jax.sharding import PartitionSpec as P

VELOCITIES = [
    (0, 0, 0),
    (1, 0, 0),
    (-1, 0, 0),
    (0, 1, 0),
    (0, -1, 0),
    (0, 0, 1),
    (0, 0, -1),
    (1, 1, 0),
    (-1, -1, 0),
    (1, -1, 0),
    (-1, 1, 0),
    (1, 0, 1),
    (-1, 0, -1),
    (1, 0, -1),
    (-1, 0, 1),
    (0, 1, 1),
    (0, -1, -1),
    (0, 1, -1),
    (0, -1, 1),
]
WEIGHTS = [1.0 / 3.0] + [1.0 / 18.0] * 6 + [1.0 / 36.0] * 12
OPPOSITE = [0, 2, 1, 4, 3, 6, 5, 8, 7, 10, 9, 12, 11, 14, 13, 16, 15, 18, 17]
coupling = 0.9
relax_times = (1.0, 0.8)
wall_values = (0.3, 1.5)


def extended(block, sides, width):
    for axis, dim in sides:
        count = lax.axis_size(axis)
        forward = [(i, i + 1) for i in range(count - 1)]
        forward.append((count - 1, 0))
        backward = [(target, source) for source, target in forward]
        low = lax.ppermute(
            lax.slice_in_dim(block, block.shape[dim] - width, None, axis=dim), axis, forward
        )
        high = lax.ppermute(lax.slice_in_dim(block, 0, width, axis=dim), axis, backward)
        block = jnp.concatenate([low, block, high], axis=dim)
    return block


def collide(populations, fluid, psi, gradient):
    vel = jnp.asarray(np.array(VELOCITIES, np.float32))
    weights = jnp.asarray(np.array(WEIGHTS, np.float32))
    rho = jnp.sum(populations, axis=1)
    moment = jnp.einsum("ia,kixyz->kaxyz", vel, populations, precision=lax.Precision.HIGHEST)
    inv_first = 1.0 / relax_times[0]
    inv_second = 1.0 / relax_times[1]
    weight_sum = rho[0] * inv_first + rho[1] * inv_second
    common = (moment[0] * inv_first + moment[1] * inv_second) / weight_sum[None]
    forces = (-coupling * psi[0][None] * gradient[1], -coupling * psi[1][None] * gradient[0])
    results = []
    for comp in range(2):
        velocity = common + relax_times[comp] * forces[comp] / rho[comp][None]
        along = jnp.einsum("ia,axyz->ixyz", vel, velocity, precision=lax.Precision.HIGHEST)
        speed_sq = jnp.sum(velocity * velocity, axis=0)
        equil = (
            weights[:, None, None, None]
            * rho[comp][None]
            * (1.0 + 3.0 * along + 4.5 * along * along - 1.5 * speed_sq[None])
        )
        current = populations[comp]
        results.append(current - (current - equil) / relax_times[comp])
    post = jnp.stack(results, axis=0)
    return jnp.where(fluid[None, None], post, populations)


def window(padded, offset, dim_first, sizes):
    out = padded
    for axis_idx in range(3):
        start = 1 + offset[axis_idx]
        out = lax.slice_in_dim(out, start, start + sizes[axis_idx], axis=dim_first + axis_idx)
    return out


def body(populations, solid):
    fluid = solid == 0
    sizes = solid.shape
    rho = jnp.sum(populations, axis=1)
    wall = jnp.asarray(np.array(wall_values, np.float32)).reshape(2, 1, 1, 1)
    psi = jnp.where(fluid[None], rho, wall)
    signed = jnp.where(fluid[None], psi, -psi)
    padded = extended(signed, (("gx", 1), ("gy", 2), ("gz", 3)), 1)
    psi_padded = jnp.abs(padded)
    fluid_padded = padded[0] > 0.0
    parts = [jnp.zeros_like(psi) for axis_idx in range(3)]
    for i in range(1, 19):
        move = VELOCITIES[i]
        beside = window(psi_padded, move, 1, sizes)
        for axis_idx in range(3):
            if move[axis_idx] != 0:
                parts[axis_idx] = parts[axis_idx] + WEIGHTS[i] * move[axis_idx] * beside
    gradient = jnp.stack(parts, axis=1)
    post = collide(populations, fluid, psi, gradient)
    halo_post = extended(post, (("gx", 2), ("gy", 3), ("gz", 4)), 1)
    pulled_all = jnp.stack(
        [
            window(
                halo_post[:, i], (-VELOCITIES[i][0], -VELOCITIES[i][1], -VELOCITIES[i][2]), 1, sizes
            )
            for i in range(19)
        ],
        axis=1,
    )
    moved = []
    for i in range(19):
        move = VELOCITIES[i]
        source_fluid = window(fluid_padded, (-move[0], -move[1], -move[2]), 0, sizes)
        moved.append(jnp.where(source_fluid[None], pulled_all[:, i], post[:, OPPOSITE[i]]))
    result = jnp.stack(moved, axis=1)
    return jnp.where(fluid[None, None], result, populations)


def solution(mesh):
    in_specs = (P(None, None, "gx", "gy", "gz"), P("gx", "gy", "gz"))
    out_specs = P(None, None, "gx", "gy", "gz")
    return jax.shard_map(body, mesh=mesh, in_specs=in_specs, out_specs=out_specs, check_vma=False)
```

profile of v0, /device:TPU:0, one launch (start us, length us, event | category | flops | bytes accessed | tf_op | source)
XLA Modules:
  0.0 80.5 jit_solution(17574721506651843226)
XLA Ops:
  0.0 0.9 %broadcast_compare_fusion = pred[4,16,128]{2,1,0:T(8,128)(4,1)S(1)} fusion(s32[4,16,128]{2,1,0:T(8,128)} %param.6), kind=kLoop, calls=%fused_computation.187 | loop fusion | flops 8192 | bytes 40960 | tf_op jit(solution)/shard_map/eq | solution.py:84
  0.9 1.4 %reduce_sum.27 = f32[2,4,16,128]{3,2,1,0:T(8,128)S(1)} reduce(f32[2,19,4,16,128]{4,3,2,1,0:T(8,128)} %param.5, f32[]{:T(128)} %constant.17.clone.1), dimensions={1}, to_apply=%region_0.0 | reduce | flops 294912 | bytes 1310724 | tf_op jit(solution)/shard_map/reduce_sum | solution.py:86
  2.3 0.1 broadcast_select_fusion
  2.4 3.0 %collective-permute-start = (f32[2,1,16,128]{3,2,1,0:T(8,128)S(1)}, f32[2,1,16,128]{3,2,1,0:T(8,128)S(1)}, u32[]{:S(2)}, u32[]{:S(2)}) collective-permute-start(f32[2,1,16,128]{3,2,1,0:T(8,128)S(1)} %get-tuple-element.49), channel_id=1, source_target_pairs={{0,8},{8,16},{16,24},{24,0},{1,9},{9,17},{17,25},{25,1},{2,10},{10... | collective-permute-start | bytes 49160 | tf_op jit(solution)/shard_map/ppermute | solution.py:41
  5.4 1.0 %collective-permute-start.1 = (f32[2,1,16,128]{3,2,1,0:T(8,128)S(1)}, f32[2,1,16,128]{3,2,1,0:T(8,128)S(1)}, u32[]{:S(2)}, u32[]{:S(2)}) collective-permute-start(f32[2,1,16,128]{3,2,1,0:T(8,128)S(1)} %get-tuple-element.50), channel_id=1, source_target_pairs={{8,0},{16,8},{24,16},{0,24},{9,1},{17,9},{25,17},{1,25},{10,2},{18... | collective-permute-start | bytes 49160 | tf_op jit(solution)/shard_map/ppermute | solution.py:44
  6.4 1.6 %convolution_bitcast_fusion = f32[2,3,4,16,128]{4,1,3,2,0:T(4,128)S(1)} fusion(f32[19,3,1,1,1]{0,1,4,3,2:T(4,128)S(1)} %copy-done.22, f32[2,19,4,16,128]{4,3,2,1,0:T(8,128)S(1)} %copy-done), kind=kOutput, calls=%fused_computation.7 | convolution fusion | flops 11206656 | bytes 1442020 | tf_op jit(solution)/shard_map/ia,kixyz->kaxyz/dot_general | solution.py:53
  8.0 1.1 %collective-permute-done.1 = f32[2,1,16,128]{3,2,1,0:T(8,128)S(1)} collective-permute-done((f32[2,1,16,128]{3,2,1,0:T(8,128)S(1)}, f32[2,1,16,128]{3,2,1,0:T(8,128)S(1)}, u32[]{:S(2)}, u32[]{:S(2)}) %collective-permute-start.1) | collective-permute-done | bytes 16416 | tf_op jit(solution)/shard_map/ppermute | solution.py:44
  9.1 0.1 collective-permute-start.2
  9.2 0.5 collective-permute-start.3
  9.7 0.7 collective-permute-done.2
  10.4 0.2 collective-permute-done.3
  10.6 0.1 fusion.108
  10.7 1.6 %collective-permute-start.4 = (f32[2,6,18,1]{3,2,1,0:T(8,128)S(1)}, f32[2,6,18,1]{3,2,1,0:T(8,128)S(1)}, u32[]{:S(2)}, u32[]{:S(2)}) collective-permute-start(f32[2,6,18,1]{3,2,1,0:T(8,128)S(1)} %get-tuple-element.38), channel_id=1, source_target_pairs={{0,1},{1,2},{2,3},{3,0},{4,5},{5,6},{6,7},{7,4},{8,9},{9,10},{10,1... | collective-permute-start | bytes 2600 | tf_op jit(solution)/shard_map/ppermute | solution.py:41
  12.3 2.2 %collective-permute-start.5 = (f32[2,6,18,1]{3,2,1,0:T(8,128)S(1)}, f32[2,6,18,1]{3,2,1,0:T(8,128)S(1)}, u32[]{:S(2)}, u32[]{:S(2)}) collective-permute-start(f32[2,6,18,1]{3,2,1,0:T(8,128)S(1)} %get-tuple-element.39), channel_id=1, source_target_pairs={{1,0},{2,1},{3,2},{0,3},{5,4},{6,5},{7,6},{4,7},{9,8},{10,9},{11,1... | collective-permute-start | bytes 2600 | tf_op jit(solution)/shard_map/ppermute | solution.py:44
  14.5 0.7 copy.36
  15.3 4.0 %collective-permute-done.4 = f32[2,6,18,1]{3,2,1,0:T(8,128)S(1)} collective-permute-done((f32[2,6,18,1]{3,2,1,0:T(8,128)S(1)}, f32[2,6,18,1]{3,2,1,0:T(8,128)S(1)}, u32[]{:S(2)}, u32[]{:S(2)}) %collective-permute-start.4) | collective-permute-done | bytes 896 | tf_op jit(solution)/shard_map/ppermute | solution.py:41
  19.3 2.0 %collective-permute-done.5 = f32[2,6,18,1]{3,2,1,0:T(8,128)S(1)} collective-permute-done((f32[2,6,18,1]{3,2,1,0:T(8,128)S(1)}, f32[2,6,18,1]{3,2,1,0:T(8,128)S(1)}, u32[]{:S(2)}, u32[]{:S(2)}) %collective-permute-start.5) | collective-permute-done | bytes 896 | tf_op jit(solution)/shard_map/ppermute | solution.py:44
  21.3 0.2 fusion.104
  21.5 0.2 fusion.92
  21.7 0.2 fusion.101
  22.0 0.2 fusion.83
  22.1 0.2 pad_maximum_fusion.3
  22.3 0.3 multiply_reduce_fusion.1
  22.6 1.1 %fusion.10 = f32[1,19,4,16,128]{4,1,3,2,0:T(8,128)S(1)} fusion(f32[2,19,4,16,128]{4,1,3,2,0:T(8,128)S(1)} %copy.36, f32[19,3,1,1]{0,1,3,2:T(4,128)S(1)} %copy-done.24, f32[3,4,16,128]{3,0,2,1:T(4,128)S(1)} %get-tuple-element.37, f32[4,16,128]{2,1,0:T(8,128)S(1)} %get-tuple-element.70, f32[4,16,128]{2,1,0:T(8,128)S(1)} %get-tuple-element.47, ...), kind=kOutput, calls=%fused_computation.18 | convolution fusion | flops 7315456 | bytes 1409328 | tf_op jit(solution)/shard_map/ia,axyz->ixyz/dot_general | solution.py:62
  23.8 1.1 %fusion.3 = f32[1,19,4,16,128]{4,1,3,2,0:T(8,128)S(1)} fusion(f32[2,19,4,16,128]{4,1,3,2,0:T(8,128)S(1)} %copy.36, f32[19,3,1,1]{0,1,3,2:T(4,128)S(1)} %copy-done.24, f32[3,4,16,128]{3,0,2,1:T(4,128)S(1)} %get-tuple-element.6, f32[4,16,128]{2,1,0:T(8,128)S(1)} %get-tuple-element.71, f32[4,16,128]{2,1,0:T(8,128)S(1)} %get-tuple-element.46, f32[19]{0:T(128)S(1)} %copy-done.25), kind=kOutput, calls=%fused_computation.11 | convolution fusion | flops 7159808 | bytes 1409328 | tf_op jit(solution)/shard_map/ia,axyz->ixyz/dot_general | solution.py:62
  24.8 0.9 %maximum_select_fusion = f32[2,19,4,16,128]{4,1,3,2,0:T(8,128)S(1)} fusion(f32[1,19,4,16,128]{4,1,3,2,0:T(8,128)S(1)} %fusion.10, f32[1,19,4,16,128]{4,1,3,2,0:T(8,128)S(1)} %fusion.3, pred[4,16,128]{2,1,0:T(8,128)(4,1)S(1)} %broadcast_compare_fusion, f32[2,19,4,16,128]{4,3,2,1,0:T(8,128)S(1)} %copy-done), kind=kLoop, calls=%fused_computation.2 | loop fusion | flops 622592 | bytes 3743744 | tf_op jit(solution)/shard_map/jit(_where)/select_n | solution.py:72
  25.7 0.2 copy.43
  26.0 2.4 %collective-permute-start.6 = (f32[2,19,1,16,128]{4,3,2,0,1:T(8,128)S(1)}, f32[2,19,1,16,128]{4,3,2,0,1:T(8,128)S(1)}, u32[]{:S(2)}, u32[]{:S(2)}) collective-permute-start(f32[2,19,1,16,128]{4,3,2,0,1:T(8,128)S(1)} %get-tuple-element.35), channel_id=1, source_target_pairs={{0,8},{8,16},{16,24},{24,0},{1,9},{9,17},{17,25},{25,1},{2,10},{10... | collective-permute-start | bytes 933896 | tf_op jit(solution)/shard_map/ppermute | solution.py:41
  28.5 0.5 collective-permute-start.7
  29.0 8.2 %collective-permute-done.6 = f32[2,19,1,16,128]{4,3,2,0,1:T(8,128)S(1)} collective-permute-done((f32[2,19,1,16,128]{4,3,2,0,1:T(8,128)S(1)}, f32[2,19,1,16,128]{4,3,2,0,1:T(8,128)S(1)}, u32[]{:S(2)}, u32[]{:S(2)}) %collective-permute-start.6) | collective-permute-done | bytes 311328 | tf_op jit(solution)/shard_map/ppermute | solution.py:41
  37.2 0.2 constant_dynamic-update-slice_fusion.1
  37.5 5.0 %collective-permute-done.7 = f32[2,19,1,16,128]{4,3,2,0,1:T(8,128)S(1)} collective-permute-done((f32[2,19,1,16,128]{4,3,2,0,1:T(8,128)S(1)}, f32[2,19,1,16,128]{4,3,2,0,1:T(8,128)S(1)}, u32[]{:S(2)}, u32[]{:S(2)}) %collective-permute-start.7) | collective-permute-done | bytes 311328 | tf_op jit(solution)/shard_map/ppermute | solution.py:44
  42.5 0.2 fusion.106
  42.7 0.5 collective-permute-start.9
  43.2 0.8 collective-permute-done.8
  44.0 0.2 collective-permute-done.9
  44.2 0.5 pad_maximum_fusion.1
  44.7 3.4 %fusion.105 = (f32[2,19,6,18,1]{4,3,2,0,1:T(8,128)}, f32[2,19,6,18,1]{4,3,2,0,1:T(8,128)}) fusion(f32[2,19,6,18,128]{4,3,2,0,1:T(8,128)S(1)} %pad_maximum_fusion.1), kind=kLoop, calls=%fused_computation.192 | loop fusion | bytes 65664 | tf_op jit(solution)/shard_map/slice | solution.py:42
  48.1 2.9 %copy.46 = f32[2,19,6,18,1]{1,0,4,3,2:T(2,128)S(1)} copy(f32[2,19,6,18,1]{4,3,2,0,1:T(8,128)} %get-tuple-element.30) | data formatting | bytes 32832 | tf_op jit(solution)/shard_map/slice | solution.py:42
  51.0 2.9 %copy.47 = f32[2,19,6,18,1]{1,0,4,3,2:T(2,128)S(1)} copy(f32[2,19,6,18,1]{4,3,2,0,1:T(8,128)} %get-tuple-element.31) | data formatting | bytes 32832 | tf_op jit(solution)/shard_map/slice | solution.py:44
  53.9 2.2 %collective-permute-start.11 = (f32[2,19,6,18,1]{1,0,4,3,2:T(2,128)S(1)}, f32[2,19,6,18,1]{1,0,4,3,2:T(2,128)}, u32[]{:S(2)}, u32[]{:S(2)}) collective-permute-start(f32[2,19,6,18,1]{1,0,4,3,2:T(2,128)S(1)} %copy.47), channel_id=1, source_target_pairs={{1,0},{2,1},{3,2},{0,3},{5,4},{6,5},{7,6},{4,7},{9,8},{10,9},{11,1... | collective-permute-start | bytes 49256 | tf_op jit(solution)/shard_map/ppermute | solution.py:44
  56.1 0.8 %fusion.110 = (pred[4,16,128]{2,1,0:T(8,128)(4,1)S(1)}, pred[4,16,128]{2,1,0:T(8,128)(4,1)S(1)}, pred[4,16,128]{2,1,0:T(8,128)(4,1)}, pred[4,16,128]{2,1,0:T(8,1...) fusion(pred[6,18,130]{2,1,0:T(8,128)(4,1)S(1)} %fusion.11), kind=kLoop, calls=%fused_computation.197 | loop fusion | bytes 311296 | tf_op jit(solution)/shard_map/slice | solution.py:79
  57.0 5.9 %collective-permute-done.10 = f32[2,19,6,18,1]{1,0,4,3,2:T(2,128)S(1)} collective-permute-done((f32[2,19,6,18,1]{1,0,4,3,2:T(2,128)S(1)}, f32[2,19,6,18,1]{1,0,4,3,2:T(2,128)S(1)}, u32[]{:S(2)}, u32[]{:S(2)}) %collective-permute-start.10) | collective-permute-done | bytes 16448 | tf_op jit(solution)/shard_map/ppermute | solution.py:41
  62.9 3.2 %copy.48 = f32[2,19,6,18,1]{4,3,2,0,1:T(8,128)} copy(f32[2,19,6,18,1]{1,0,4,3,2:T(2,128)S(1)} %collective-permute-done.10) | data formatting | bytes 32832 | tf_op jit(solution)/shard_map/ppermute | solution.py:41
  66.1 4.1 %copy.49 = f32[2,19,6,18,1]{4,3,2,0,1:T(8,128)} copy(f32[2,19,6,18,1]{1,0,4,3,2:T(2,128)} %collective-permute-done.11) | data formatting | bytes 32832 | tf_op jit(solution)/shard_map/ppermute | solution.py:44
  70.3 6.0 %pad_maximum_fusion = f32[2,19,6,18,130]{4,3,2,0,1:T(8,128)S(1)} fusion(f32[2,19,6,18,1]{4,3,2,0,1:T(8,128)} %copy.49, f32[2,19,6,1,128]{4,3,2,0,1:T(1,128)S(1)} %collective-permute-done.9, f32[2,19,6,16,128]{4,3,2,0,1:T(8,128)S(1)} %copy-done.2, f32[2,19,6,1,128]{4,3,2,0,1:T(1,128)S(1)} %collective-permute-done.8, f32[2,19,6,18,1]{4,3,2,0,1:T(8,128)} %copy.48), kind=kLoop, calls=%fused_computation | loop fusion | flops 2134080 | bytes 4268160 | tf_op jit(solution)/shard_map/concatenate | solution.py:45
  76.3 0.6 slice_bitcast_fusion.2
  77.0 0.6 copy-done.4
  77.6 0.1 fusion.74
  77.7 0.1 fusion.71
  77.8 0.1 fusion.68
  77.9 0.1 fusion.65
  78.0 0.1 fusion.62
  78.2 0.1 fusion.56
  78.3 0.1 fusion.53
  78.4 0.1 fusion.50
  78.5 0.1 fusion.47
  78.6 0.1 fusion.44
  78.7 0.1 fusion.38
  78.8 0.1 fusion.35
  79.0 0.1 fusion.26
  79.1 0.1 fusion.23
  79.2 0.2 copy_select_fusion
  79.4 1.1 %copy.69 = f32[2,19,4,16,128]{4,3,2,1,0:T(8,128)} copy(f32[2,19,4,16,128]{4,3,2,0,1:T(8,128)S(1)} %copy_select_fusion) | data formatting | bytes 2490368 | tf_op jit(solution)/shard_map/jit(_where)/select_n | solution.py:118
  (71 shorter events, 0.5 us)
Async XLA Ops:
  0.0 2.2 %copy-start.23 = (f32[2]{0:T(128)S(1)}, f32[2]{0:T(128)}, u32[]{:S(2)}) copy-start(f32[2]{0:T(128)} %constant.14.clone) | copy-start | bytes 28
  0.0 6.4 %copy-start.22 = (f32[19,3,1,1,1]{0,1,4,3,2:T(4,128)S(1)}, f32[19,3,1,1,1]{0,1,4,3,2:T(4,128)}, u32[]{:S(2)}) copy-start(f32[19,3,1,1,1]{0,1,4,3,2:T(4,128)} %constant.40) | copy-start | bytes 688
  0.0 6.4 %copy-start = (f32[2,19,4,16,128]{4,3,2,1,0:T(8,128)S(1)}, f32[2,19,4,16,128]{4,3,2,1,0:T(8,128)}, u32[]{:S(2)}) copy-start(f32[2,19,4,16,128]{4,3,2,1,0:T(8,128)} %param.5) | copy-start | bytes 3735556
  2.4 5.7 %collective-permute-start = (f32[2,1,16,128]{3,2,1,0:T(8,128)S(1)}, f32[2,1,16,128]{3,2,1,0:T(8,128)S(1)}, u32[]{:S(2)}, u32[]{:S(2)}) collective-permute-start(f32[2,1,16,128]{3,2,1,0:T(8,128)S(1)} %get-tuple-element.49), channel_id=1, source_target_pairs={{0,8},{8,16},{16,24},{24,0},{1,9},{9,17},{17,25},{25,1},{2,10},{10... | collective-permute-start | bytes 49160 | tf_op jit(solution)/shard_map/ppermute | solution.py:41
  5.4 3.7 %collective-permute-start.1 = (f32[2,1,16,128]{3,2,1,0:T(8,128)S(1)}, f32[2,1,16,128]{3,2,1,0:T(8,128)S(1)}, u32[]{:S(2)}, u32[]{:S(2)}) collective-permute-start(f32[2,1,16,128]{3,2,1,0:T(8,128)S(1)} %get-tuple-element.50), channel_id=1, source_target_pairs={{8,0},{16,8},{24,16},{0,24},{9,1},{17,9},{25,17},{1,25},{10,2},{18... | collective-permute-start | bytes 49160 | tf_op jit(solution)/shard_map/ppermute | solution.py:44
  9.1 1.2 %collective-permute-start.2 = (f32[2,6,1,128]{3,2,1,0:T(1,128)S(1)}, f32[2,6,1,128]{3,2,1,0:T(1,128)S(1)}, u32[]{:S(2)}, u32[]{:S(2)}) collective-permute-start(f32[2,6,1,128]{3,2,1,0:T(1,128)S(1)} %get-tuple-element.40), channel_id=1, source_target_pairs={{0,4},{4,0},{1,5},{5,1},{2,6},{6,2},{3,7},{7,3},{8,12},{12,8},{9,1... | collective-permute-start | bytes 18440 | tf_op jit(solution)/shard_map/ppermute | solution.py:41
  9.2 1.3 %collective-permute-start.3 = (f32[2,6,1,128]{3,2,1,0:T(1,128)S(1)}, f32[2,6,1,128]{3,2,1,0:T(1,128)S(1)}, u32[]{:S(2)}, u32[]{:S(2)}) collective-permute-start(f32[2,6,1,128]{3,2,1,0:T(1,128)S(1)} %get-tuple-element.41), channel_id=1, source_target_pairs={{4,0},{0,4},{5,1},{1,5},{6,2},{2,6},{7,3},{3,7},{12,8},{8,12},{13,... | collective-permute-start | bytes 18440 | tf_op jit(solution)/shard_map/ppermute | solution.py:44
  10.7 8.6 %collective-permute-start.4 = (f32[2,6,18,1]{3,2,1,0:T(8,128)S(1)}, f32[2,6,18,1]{3,2,1,0:T(8,128)S(1)}, u32[]{:S(2)}, u32[]{:S(2)}) collective-permute-start(f32[2,6,18,1]{3,2,1,0:T(8,128)S(1)} %get-tuple-element.38), channel_id=1, source_target_pairs={{0,1},{1,2},{2,3},{3,0},{4,5},{5,6},{6,7},{7,4},{8,9},{9,10},{10,1... | collective-permute-start | bytes 2600 | tf_op jit(solution)/shard_map/ppermute | solution.py:41
  12.3 9.0 %collective-permute-start.5 = (f32[2,6,18,1]{3,2,1,0:T(8,128)S(1)}, f32[2,6,18,1]{3,2,1,0:T(8,128)S(1)}, u32[]{:S(2)}, u32[]{:S(2)}) collective-permute-start(f32[2,6,18,1]{3,2,1,0:T(8,128)S(1)} %get-tuple-element.39), channel_id=1, source_target_pairs={{1,0},{2,1},{3,2},{0,3},{5,4},{6,5},{7,6},{4,7},{9,8},{10,9},{11,1... | collective-permute-start | bytes 2600 | tf_op jit(solution)/shard_map/ppermute | solution.py:44
  21.9 0.7 copy-start.24
  21.9 0.7 copy-start.25
  26.0 11.5 %copy-start.3 = (f32[2,19,4,16,128]{4,3,2,0,1:T(8,128)}, f32[2,19,4,16,128]{4,3,2,0,1:T(8,128)S(1)}, u32[]{:S(2)}) copy-start(f32[2,19,4,16,128]{4,3,2,0,1:T(8,128)S(1)} %copy.43) | copy-start | bytes 3735556
  26.0 11.2 %collective-permute-start.6 = (f32[2,19,1,16,128]{4,3,2,0,1:T(8,128)S(1)}, f32[2,19,1,16,128]{4,3,2,0,1:T(8,128)S(1)}, u32[]{:S(2)}, u32[]{:S(2)}) collective-permute-start(f32[2,19,1,16,128]{4,3,2,0,1:T(8,128)S(1)} %get-tuple-element.35), channel_id=1, source_target_pairs={{0,8},{8,16},{16,24},{24,0},{1,9},{9,17},{17,25},{25,1},{2,10},{10... | collective-permute-start | bytes 933896 | tf_op jit(solution)/shard_map/ppermute | solution.py:41
  28.5 13.9 %collective-permute-start.7 = (f32[2,19,1,16,128]{4,3,2,0,1:T(8,128)S(1)}, f32[2,19,1,16,128]{4,3,2,0,1:T(8,128)S(1)}, u32[]{:S(2)}, u32[]{:S(2)}) collective-permute-start(f32[2,19,1,16,128]{4,3,2,0,1:T(8,128)S(1)} %get-tuple-element.34), channel_id=1, source_target_pairs={{8,0},{16,8},{24,16},{0,24},{9,1},{17,9},{25,17},{1,25},{10,2},{18... | collective-permute-start | bytes 933896 | tf_op jit(solution)/shard_map/ppermute | solution.py:44
  42.4 1.7 %copy-start.1 = (f32[2,19,6,16,128]{4,3,2,0,1:T(8,128)}, f32[2,19,6,16,128]{4,3,2,0,1:T(8,128)S(1)}, u32[]{:S(2)}) copy-start(f32[2,19,6,16,128]{4,3,2,0,1:T(8,128)S(1)} %constant_dynamic-update-slice_fusion) | copy-start | bytes 5603332
  42.6 1.4 %collective-permute-start.8 = (f32[2,19,6,1,128]{4,3,2,0,1:T(1,128)S(1)}, f32[2,19,6,1,128]{4,3,2,0,1:T(1,128)S(1)}, u32[]{:S(2)}, u32[]{:S(2)}) collective-permute-start(f32[2,19,6,1,128]{4,3,2,0,1:T(1,128)S(1)} %get-tuple-element.32), channel_id=1, source_target_pairs={{0,4},{4,0},{1,5},{5,1},{2,6},{6,2},{3,7},{7,3},{8,12},{12,8},{9,1... | collective-permute-start | bytes 350216 | tf_op jit(solution)/shard_map/ppermute | solution.py:41
  42.7 1.5 %collective-permute-start.9 = (f32[2,19,6,1,128]{4,3,2,0,1:T(1,128)S(1)}, f32[2,19,6,1,128]{4,3,2,0,1:T(1,128)S(1)}, u32[]{:S(2)}, u32[]{:S(2)}) collective-permute-start(f32[2,19,6,1,128]{4,3,2,0,1:T(1,128)S(1)} %get-tuple-element.33), channel_id=1, source_target_pairs={{4,0},{0,4},{5,1},{1,5},{6,2},{2,6},{7,3},{3,7},{12,8},{8,12},{13,... | collective-permute-start | bytes 350216 | tf_op jit(solution)/shard_map/ppermute | solution.py:44
  53.9 12.3 %collective-permute-start.11 = (f32[2,19,6,18,1]{1,0,4,3,2:T(2,128)S(1)}, f32[2,19,6,18,1]{1,0,4,3,2:T(2,128)}, u32[]{:S(2)}, u32[]{:S(2)}) collective-permute-start(f32[2,19,6,18,1]{1,0,4,3,2:T(2,128)S(1)} %copy.47), channel_id=1, source_target_pairs={{1,0},{2,1},{3,2},{0,3},{5,4},{6,5},{7,6},{4,7},{9,8},{10,9},{11,1... | collective-permute-start | bytes 49256 | tf_op jit(solution)/shard_map/ppermute | solution.py:44
  56.1 6.8 %collective-permute-start.10 = (f32[2,19,6,18,1]{1,0,4,3,2:T(2,128)S(1)}, f32[2,19,6,18,1]{1,0,4,3,2:T(2,128)S(1)}, u32[]{:S(2)}, u32[]{:S(2)}) collective-permute-start(f32[2,19,6,18,1]{1,0,4,3,2:T(2,128)S(1)} %copy.46), channel_id=1, source_target_pairs={{0,1},{1,2},{2,3},{3,0},{4,5},{5,6},{6,7},{7,4},{8,9},{9,10},{10,1... | collective-permute-start | bytes 49256 | tf_op jit(solution)/shard_map/ppermute | solution.py:41
  66.1 4.2 %copy-start.2 = (f32[2,19,6,16,128]{4,3,2,0,1:T(8,128)S(1)}, f32[2,19,6,16,128]{4,3,2,0,1:T(8,128)}, u32[]{:S(2)}) copy-start(f32[2,19,6,16,128]{4,3,2,0,1:T(8,128)} %copy-done.1) | copy-start | bytes 5603332
  76.3 1.3 %copy-start.4 = (f32[2,19,4,16,128]{4,3,2,0,1:T(8,128)S(1)}, f32[2,19,4,16,128]{4,3,2,0,1:T(8,128)}, u32[]{:S(2)}) copy-start(f32[2,19,4,16,128]{4,3,2,0,1:T(8,128)} %copy-done.3) | copy-start | bytes 3735556
  76.3 1.3 %copy-start.21 = (pred[4,16,128]{2,1,0:T(8,128)(4,1)S(1)}, pred[4,16,128]{2,1,0:T(8,128)(4,1)}, u32[]{:S(2)}) copy-start(pred[4,16,128]{2,1,0:T(8,128)(4,1)} %get-tuple-element.69) | copy-start | bytes 24580
  76.3 1.4 %copy-start.20 = (pred[4,16,128]{2,1,0:T(8,128)(4,1)S(1)}, pred[4,16,128]{2,1,0:T(8,128)(4,1)}, u32[]{:S(2)}) copy-start(pred[4,16,128]{2,1,0:T(8,128)(4,1)} %get-tuple-element.68) | copy-start | bytes 24580
  76.3 1.5 %copy-start.19 = (pred[4,16,128]{2,1,0:T(8,128)(4,1)S(1)}, pred[4,16,128]{2,1,0:T(8,128)(4,1)}, u32[]{:S(2)}) copy-start(pred[4,16,128]{2,1,0:T(8,128)(4,1)} %get-tuple-element.67) | copy-start | bytes 24580
  76.3 1.6 %copy-start.18 = (pred[4,16,128]{2,1,0:T(8,128)(4,1)S(1)}, pred[4,16,128]{2,1,0:T(8,128)(4,1)}, u32[]{:S(2)}) copy-start(pred[4,16,128]{2,1,0:T(8,128)(4,1)} %get-tuple-element.66) | copy-start | bytes 24580
  76.3 1.7 %copy-start.17 = (pred[4,16,128]{2,1,0:T(8,128)(4,1)S(1)}, pred[4,16,128]{2,1,0:T(8,128)(4,1)}, u32[]{:S(2)}) copy-start(pred[4,16,128]{2,1,0:T(8,128)(4,1)} %get-tuple-element.65) | copy-start | bytes 24580
  76.3 1.8 %copy-start.16 = (pred[4,16,128]{2,1,0:T(8,128)(4,1)S(1)}, pred[4,16,128]{2,1,0:T(8,128)(4,1)}, u32[]{:S(2)}) copy-start(pred[4,16,128]{2,1,0:T(8,128)(4,1)} %get-tuple-element.64) | copy-start | bytes 24580
  76.9 1.2 %copy-start.15 = (pred[4,16,128]{2,1,0:T(8,128)(4,1)S(1)}, pred[4,16,128]{2,1,0:T(8,128)(4,1)}, u32[]{:S(2)}) copy-start(pred[4,16,128]{2,1,0:T(8,128)(4,1)} %get-tuple-element.63) | copy-start | bytes 24580
  77.0 1.3 %copy-start.14 = (pred[4,16,128]{2,1,0:T(8,128)(4,1)S(1)}, pred[4,16,128]{2,1,0:T(8,128)(4,1)}, u32[]{:S(2)}) copy-start(pred[4,16,128]{2,1,0:T(8,128)(4,1)} %get-tuple-element.62) | copy-start | bytes 24580
  77.0 1.4 %copy-start.13 = (pred[4,16,128]{2,1,0:T(8,128)(4,1)S(1)}, pred[4,16,128]{2,1,0:T(8,128)(4,1)}, u32[]{:S(2)}) copy-start(pred[4,16,128]{2,1,0:T(8,128)(4,1)} %get-tuple-element.61) | copy-start | bytes 24580
  77.0 1.5 %copy-start.12 = (pred[4,16,128]{2,1,0:T(8,128)(4,1)S(1)}, pred[4,16,128]{2,1,0:T(8,128)(4,1)}, u32[]{:S(2)}) copy-start(pred[4,16,128]{2,1,0:T(8,128)(4,1)} %get-tuple-element.60) | copy-start | bytes 24580
  77.0 1.6 %copy-start.11 = (pred[4,16,128]{2,1,0:T(8,128)(4,1)S(1)}, pred[4,16,128]{2,1,0:T(8,128)(4,1)}, u32[]{:S(2)}) copy-start(pred[4,16,128]{2,1,0:T(8,128)(4,1)} %get-tuple-element.59) | copy-start | bytes 24580
  77.0 1.7 %copy-start.10 = (pred[4,16,128]{2,1,0:T(8,128)(4,1)S(1)}, pred[4,16,128]{2,1,0:T(8,128)(4,1)}, u32[]{:S(2)}) copy-start(pred[4,16,128]{2,1,0:T(8,128)(4,1)} %get-tuple-element.58) | copy-start | bytes 24580
  77.6 1.1 %copy-start.9 = (pred[4,16,128]{2,1,0:T(8,128)(4,1)S(1)}, pred[4,16,128]{2,1,0:T(8,128)(4,1)}, u32[]{:S(2)}) copy-start(pred[4,16,128]{2,1,0:T(8,128)(4,1)} %get-tuple-element.57) | copy-start | bytes 24580
  77.7 1.1 %copy-start.8 = (pred[4,16,128]{2,1,0:T(8,128)(4,1)S(1)}, pred[4,16,128]{2,1,0:T(8,128)(4,1)}, u32[]{:S(2)}) copy-start(pred[4,16,128]{2,1,0:T(8,128)(4,1)} %get-tuple-element.56) | copy-start | bytes 24580
  77.8 1.1 %copy-start.7 = (pred[4,16,128]{2,1,0:T(8,128)(4,1)S(1)}, pred[4,16,128]{2,1,0:T(8,128)(4,1)}, u32[]{:S(2)}) copy-start(pred[4,16,128]{2,1,0:T(8,128)(4,1)} %get-tuple-element.55) | copy-start | bytes 24580
  77.9 1.0 %copy-start.6 = (pred[4,16,128]{2,1,0:T(8,128)(4,1)S(1)}, pred[4,16,128]{2,1,0:T(8,128)(4,1)}, u32[]{:S(2)}) copy-start(pred[4,16,128]{2,1,0:T(8,128)(4,1)} %get-tuple-element.54) | copy-start | bytes 24580
  78.0 0.9 %copy-start.5 = (pred[4,16,128]{2,1,0:T(8,128)(4,1)S(1)}, pred[4,16,128]{2,1,0:T(8,128)(4,1)}, u32[]{:S(2)}) copy-start(pred[4,16,128]{2,1,0:T(8,128)(4,1)} %get-tuple-element.53) | copy-start | bytes 24580
where the time goes:
time: 80.7 us; the launch traced here: 80.5 us
  waiting for transfers between devices  27.9 us (35%)
  local copies, waits for them, and re-layouts  21.3 us (26%)
  starting transfers between devices  14.3 us (18%)
  other arithmetic  12.5 us (15%)
  matrix products  3.77 us (5%)
    ppermute x6, waiting for transfers between devices, extended(): lax.ppermute(lax.slice_in_dim(block, block.shape[dim] - width, None, axis...  19.6 us
    ppermute x6, waiting for transfers between devices, extended(): lax.ppermute(lax.slice_in_dim(block, 0, width, axis=dim), axis, backward)  8.34 us
    ppermute x6, starting transfers between devices, extended(): lax.ppermute(lax.slice_in_dim(block, block.shape[dim] - width, None, axis...  7.24 us
    ppermute x6, starting transfers between devices, extended(): lax.ppermute(lax.slice_in_dim(block, 0, width, axis=dim), axis, backward)  7.01 us
    slice x5, local copies, waits for them, and re-layouts, extended(): lax.slice_in_dim(block, block.shape[dim] - width, None, axis=dim)  6.56 us
    concatenate x3, other arithmetic, extended(): block = jnp.concatenate([low, block, high], axis=dim)  6.5 us
    ppermute x1, local copies, waits for them, and re-layouts, extended(): lax.ppermute(lax.slice_in_dim(block, 0, width, axis=dim), axis, backward)  4.15 us
    ppermute x1, local copies, waits for them, and re-layouts, extended(): lax.ppermute(lax.slice_in_dim(block, block.shape[dim] - width, None, axis...  3.21 us
  transfers between devices with their start and end apart: 12, of which 10 were waited for; matrix products, arithmetic and copies ran while one was open for 8% of the time, Pallas kernels for 0%

commit v1 on v0

v1 whole, which is shorter than its diff:
```python
import functools

import jax
import jax.numpy as jnp
from jax import lax
from jax.experimental import pallas as pl
from jax.experimental.pallas import tpu as pltpu
from jax.sharding import PartitionSpec as P

VEL = [
    (0, 0, 0),
    (1, 0, 0), (-1, 0, 0), (0, 1, 0), (0, -1, 0), (0, 0, 1), (0, 0, -1),
    (1, 1, 0), (-1, -1, 0), (1, -1, 0), (-1, 1, 0),
    (1, 0, 1), (-1, 0, -1), (1, 0, -1), (-1, 0, 1),
    (0, 1, 1), (0, -1, -1), (0, 1, -1), (0, -1, 1),
]
WEIGHT = [1.0 / 3.0] + [1.0 / 18.0] * 6 + [1.0 / 36.0] * 12
OPP = [0, 2, 1, 4, 3, 6, 5, 8, 7, 10, 9, 12, 11, 14, 13, 16, 15, 18, 17]
COUPLING = 0.9
TAU = (1.0, 0.8)
WALL = (0.3, 1.5)
W1, W2 = 1.0 / 18.0, 1.0 / 36.0
BLOCKED = 1e30
LIMIT = 1e29

XP = [i for i in range(19) if VEL[i][0] == 1]
XM = [i for i in range(19) if VEL[i][0] == -1]
ZP = [i for i in range(19) if VEL[i][2] == 1]
ZM = [i for i in range(19) if VEL[i][2] == -1]
YP = [i for i in range(19) if VEL[i][1] == 1]
YPAIR = [(i, VEL.index((VEL[i][0], -1, VEL[i][2]))) for i in YP]
HALO = 12


def lanes(shape):
    return lax.broadcasted_iota(jnp.int32, shape, len(shape) - 1)


def roll(v, shift, axis):
    shift = shift % v.shape[axis]
    return pltpu.roll(v, shift, axis) if shift else v


def up(v):
    return roll(v, -1, 0)


def down(v):
    return roll(v, 1, 0)


def fold(v, rows):
    tile = lax.broadcasted_iota(jnp.int32, (8, v.shape[1]), 0)
    return jnp.where(tile < 4, v[:8], v[rows - 8 : rows])


def parity(axis):
    return lax.rem(lax.axis_index(axis), 2) == 0


def put(sheet, value, source, target):
    return jnp.where(lanes(sheet.shape) == target, roll(value, target - source, 1), sheet)


def y_index(nx):
    wide, mid = nx + 4, nx + 2
    psi = lambda k, x: k * wide + x + 2
    com = lambda a, x: 2 * wide + a * mid + x + 1
    base = 2 * wide + 3 * mid
    pair = lambda j, x: base + j * nx + x
    low, high = base + 5 * nx, base + 5 * nx + 1
    return psi, com, pair, low, high, high + 1


def first_kernel(pop, solid, field, send_a, send_b, rows_out, sheets):
    nx, ny, nz = solid.shape
    wide = nx + 4
    psi, com, pair, _, _, _ = y_index(nx)
    for x in range(nx):
        fluid = solid[x] == 0
        q = []
        rho0 = rho1 = None
        for i in range(19):
            p0, p1 = pop[0, i, x], pop[1, i, x]
            rho0 = p0 if rho0 is None else rho0 + p0
            rho1 = p1 if rho1 is None else rho1 + p1
            q.append(p0 * (1.0 / TAU[0]) + p1 * (1.0 / TAU[1]))
        inverse = 1.0 / (rho0 * (1.0 / TAU[0]) + rho1 * (1.0 / TAU[1]))
        values = [jnp.where(fluid, rho0, -WALL[0]), jnp.where(fluid, rho1, -WALL[1])]
        for a in range(3):
            total = None
            for i in range(1, 19):
                if VEL[i][a] == 1:
                    term = q[i] - q[OPP[i]]
                    total = term if total is None else total + term
            values.append(total * inverse)
        for f in range(5):
            field[f, x] = values[f]
            rows_out[psi(f, x) if f < 2 else com(f - 2, x)] = fold(values[f], ny)
        for j, (plus, minus) in enumerate(YPAIR):
            tile = lax.broadcasted_iota(jnp.int32, (8, nz), 0)
            rows_out[pair(j, x)] = jnp.where(tile < 4, pop[1, minus, x, 0:8], pop[1, plus, x, ny - 8 : ny])
    even = parity("gx")
    high = [field[f, nx - 1] for f in range(5)] + [pop[1, i, nx - 1] for i in XP] + [field[f, nx - 2] for f in range(2)]
    low = [field[f, 0] for f in range(5)] + [pop[1, i, 0] for i in XM] + [field[f, 1] for f in range(2)]
    for f in range(HALO):
        send_a[f] = jnp.where(even, high[f], low[f])
        send_b[f] = jnp.where(even, low[f], high[f])
    for side, edge, inner, dirs in ((0, nz - 1, nz - 2, ZP), (1, 0, 1, ZM)):
        sheet = jnp.zeros((ny, nz), jnp.float32)
        for x in range(nx):
            for f in range(5):
                sheet = put(sheet, field[f, x], edge, f * wide + x + 2)
            for j, i in enumerate(dirs):
                sheet = put(sheet, pop[1, i, x], edge, (5 + j) * wide + x + 2)
            for k in range(2):
                sheet = put(sheet, field[k, x], inner, (10 + k) * wide + x + 2)
        sheets[side] = sheet


def sides(even, from_a, from_b, f):
    a, b = from_a[f], from_b[f]
    return jnp.where(even, a, b), jnp.where(even, b, a)


def y_kernel(nx, rows_in, from_a, from_b, rows_out):
    psi, com, pair, low, high, count = y_index(nx)
    ny = from_a.shape[1]
    even = parity("gx")
    for k in range(2):
        for x in range(nx):
            rows_out[psi(k, x)] = rows_in[psi(k, x)]
        above, below = sides(even, from_a, from_b, k)
        rows_out[psi(k, nx)], rows_out[psi(k, -1)] = fold(above, ny), fold(below, ny)
        above, below = sides(even, from_a, from_b, 10 + k)
        rows_out[psi(k, nx + 1)], rows_out[psi(k, -2)] = fold(above, ny), fold(below, ny)
    for a in range(3):
        for x in range(nx):
            rows_out[com(a, x)] = rows_in[com(a, x)]
        above, below = sides(even, from_a, from_b, 2 + a)
        rows_out[com(a, nx)], rows_out[com(a, -1)] = fold(above, ny), fold(below, ny)
    for j in range(5):
        for x in range(nx):
            rows_out[pair(j, x)] = rows_in[pair(j, x)]
    tile = lax.broadcasted_iota(jnp.int32, (8, from_a.shape[2]), 0)
    for where, step, dirs in ((low, 1, XP), (high, -1, XM)):
        plus, minus = dirs.index(VEL.index((step, 1, 0))) + 5, dirs.index(VEL.index((step, -1, 0))) + 5
        take = 1 if step == 1 else 0
        top, bottom = sides(even, from_a, from_b, minus)[take], sides(even, from_a, from_b, plus)[take]
        rows_out[where] = jnp.where(tile < 4, top[:8], bottom[ny - 8 :])


def merge_rows(y_even, from_y, n):
    if len(from_y) == 1:
        return from_y[0][n]
    a, b = from_y[0][n], from_y[1][n]
    tile = lax.broadcasted_iota(jnp.int32, a.shape, 0)
    return jnp.where((tile < 4) == y_even, a, b)


def z_kernel(nx, y_parts, sheets, from_a, from_b, *rest):
    from_y, (send_a, send_b) = rest[:y_parts], rest[y_parts:]
    psi, com, pair, low, high, _ = y_index(nx)
    wide = nx + 4
    nz = from_a.shape[2]
    x_even, y_even, z_even = parity("gx"), parity("gy"), parity("gz")
    rows = lambda n: merge_rows(y_even, from_y, n)
    above = lambda f: sides(x_even, from_a, from_b, f)[0]
    below = lambda f: sides(x_even, from_a, from_b, f)[1]
    made = []
    for side, edge, inner, dirs, cz in ((0, nz - 1, nz - 2, ZP, 1), (1, 0, 1, ZM, -1)):
        main = sheets[side]
        halo = jnp.zeros((8, nz), jnp.float32)
        for k in range(2):
            for f, lane in ((k, edge), (10 + k, inner)):
                main = put(main, below(k), lane, f * wide + 1)
                main = put(main, below(10 + k), lane, f * wide)
                main = put(main, above(k), lane, f * wide + nx + 2)
                main = put(main, above(10 + k), lane, f * wide + nx + 3)
                for x in range(-2, nx + 2):
                    halo = put(halo, rows(psi(k, x)), lane, f * wide + x + 2)
        for a in range(3):
            main = put(main, below(2 + a), edge, (2 + a) * wide + 1)
            main = put(main, above(2 + a), edge, (2 + a) * wide + nx + 2)
            for x in range(-1, nx + 1):
                halo = put(halo, rows(com(a, x)), edge, (2 + a) * wide + x + 2)
        for step, half, xs, source in ((1, XP, 1, below), (-1, XM, nx + 2, above)):
            i = VEL.index((step, 0, cz))
            main = put(main, source(5 + half.index(i)), edge, (5 + dirs.index(i)) * wide + xs)
        for j, (plus, minus) in enumerate(YPAIR):
            if VEL[plus][2] == cz:
                for x in range(nx):
                    tile = rows(pair(j, x))
                    halo = put(halo, tile, edge, (5 + dirs.index(plus)) * wide + x + 2)
                    halo = put(halo, tile, edge, (5 + dirs.index(minus)) * wide + x + 2)
        made.append(jnp.concatenate([main, halo], axis=0))
    send_a[...] = jnp.where(z_even, made[0], made[1])
    send_b[...] = jnp.where(z_even, made[1], made[0])


def posts(rho, vel, fluid, dirs, pop):
    out = {}
    for k in range(2):
        u = vel[k]
        base = rho[k] * (1.0 - 1.5 * (u[0] * u[0] + u[1] * u[1] + u[2] * u[2]))
        for i in dirs:
            rows = pop(k, i, True)
            cut = (lambda v: v[:rows]) if rows != rho[k].shape[0] else (lambda v: v)
            if i == 0:
                equil = base * WEIGHT[0]
            else:
                lead = next(a for a in range(3) if VEL[i][a])
                main = i if VEL[i][lead] == 1 else OPP[i]
                along = None
                for a in range(3):
                    c = VEL[main][a]
                    if c:
                        along = u[a] if along is None else (along + u[a] if c == 1 else along - u[a])
                flow = rho[k] * along
                even = base * WEIGHT[i] + (4.5 * WEIGHT[i]) * (flow * along)
                odd = (3.0 * WEIGHT[i]) * flow
                equil = even + odd if main == i else even - odd
            equil = cut(equil)
            if k == 0:
                post = equil
            else:
                post = (1.0 / TAU[1]) * equil + (1.0 - 1.0 / TAU[1]) * pop(k, i, False)
            out[k, i] = jnp.where(cut(fluid), post, BLOCKED)
    return out


def last_kernel(nx, y_parts, pop, solid, field, from_a, from_b, own_a, own_b, zf_a, zf_b, *rest):
    from_y, (out, t_ref, dy_ref, dz_ref, gy_ref, gz_ref, post_ref, edge_ref) = rest[:y_parts], rest[y_parts:]
    psi, com, pair, low, high, _ = y_index(nx)
    wide = nx + 4
    ny, nz = from_a.shape[1:]
    x_even, y_even, z_even = parity("gx"), parity("gy"), parity("gz")
    rows = lambda n: merge_rows(y_even, from_y, n)
    above = lambda f: sides(x_even, from_a, from_b, f)[0]
    below = lambda f: sides(x_even, from_a, from_b, f)[1]
    own_hi, own_lo = jnp.where(z_even, own_a[...], own_b[...]), jnp.where(z_even, own_b[...], own_a[...])
    z_hi, z_lo = jnp.where(z_even, zf_a[...], zf_b[...]), jnp.where(z_even, zf_b[...], zf_a[...])
    tall = (ny + 8, nz)

    def signed(k, x):
        if x < 0:
            main = below(k if x == -1 else 10 + k)
        elif x >= nx:
            main = above(k if x == nx else 10 + k)
        else:
            main = field[k, x]
        return jnp.concatenate([main, rows(psi(k, x))], axis=0)

    lane = lanes(tall)
    for k in range(2):
        for x in range(-2, nx + 2):
            a = jnp.abs(signed(k, x))
            column = k * wide + x + 2
            minus = jnp.where(lane == 0, jnp.abs(roll(z_lo, -column, 1)), roll(a, 1, 1))
            plus = jnp.where(lane == nz - 1, jnp.abs(roll(z_hi, nz - 1 - column, 1)), roll(a, -1, 1))
            a_up, a_down = up(a), down(a)
            z_sum, dz, dy = plus + minus, plus - minus, a_up - a_down
            t_ref[k, x + 2] = W1 * a + W2 * (a_up + a_down + z_sum)
            dy_ref[k, x + 2] = dy
            dz_ref[k, x + 2] = dz
            if -2 < x < nx + 1:
                gy_ref[k, x + 1] = W1 * dy + W2 * (up(z_sum) - down(z_sum))
                gz_ref[k, x + 1] = W1 * dz + W2 * (up(dz) + down(dz))

    for x in range(-1, nx + 1):
        gradient = []
        for k in range(2):
            gradient.append((
                t_ref[k, x + 3] - t_ref[k, x + 1],
                gy_ref[k, x + 1] + W2 * (dy_ref[k, x + 3] + dy_ref[k, x + 1]),
                gz_ref[k, x + 1] + W2 * (dz_ref[k, x + 3] + dz_ref[k, x + 1]),
            ))
        common = []
        for a in range(3):
            main = below(2 + a) if x < 0 else above(2 + a) if x == nx else field[2 + a, x]
            common.append(jnp.concatenate([main, rows(com(a, x))], axis=0))
        vel = [[common[a] - (COUPLING * TAU[k]) * gradient[1 - k][a] for a in range(3)] for k in range(2)]
        s0, s1 = signed(0, x), signed(1, x)

        def population(k, i, ask, x=x):
            if ask:
                return ny + 8 if VEL[i][1] else ny
            if x < 0:
                main = below(5 + XP.index(i))
            elif x == nx:
                main = above(5 + XM.index(i))
            else:
                main = pop[1, i, x]
            if not VEL[i][1]:
                return main
            j = next(j for j, both in enumerate(YPAIR) if i in both)
            return jnp.concatenate([main, rows(low if x < 0 else high if x == nx else pair(j, x))], axis=0)

        dirs = XP if x < 0 else XM if x == nx else range(19)
        for (k, i), value in posts((jnp.abs(s0), jnp.abs(s1)), vel, s0 > 0.0, dirs, population).items():
            post_ref[k, i, x + 1, 0 : value.shape[0]] = value

    for side, sheet, own, dirs in ((0, z_lo, own_lo, ZP), (1, z_hi, own_hi, ZM)):
        part = lambda s, f: roll(s, -f * wide, 1)
        gradient, sign = [], [part(sheet, 0), part(sheet, 1)]
        for k in range(2):
            a, beyond, inside = jnp.abs(sign[k]), jnp.abs(part(sheet, 10 + k)), jnp.abs(part(own, k))
            plus, minus = (inside, beyond) if side == 0 else (beyond, inside)
            a_up, a_down = up(a), down(a)
            z_sum, dz, dy = plus + minus, plus - minus, a_up - a_down
            t = W1 * a + W2 * (a_up + a_down + z_sum)
            right, left = (lambda v: roll(v, -1, 1)), (lambda v: roll(v, 1, 1))
            gradient.append((
                right(t) - left(t),
                W1 * dy + W2 * (up(z_sum) - down(z_sum) + right(dy) + left(dy)),
                W1 * dz + W2 * (up(dz) + down(dz) + right(dz) + left(dz)),
            ))
        common = [part(sheet, 2 + a) for a in range(3)]
        vel = [[common[a] - (COUPLING * TAU[k]) * gradient[1 - k][a] for a in range(3)] for k in range(2)]
        rho = (jnp.abs(sign[0]), jnp.abs(sign[1]))
        population = lambda k, i, ask: ny + 8 if ask else part(sheet, 5 + dirs.index(i))
        for (k, i), value in posts(rho, vel, sign[0] > 0.0, dirs, population).items():
            edge_ref[k, side, dirs.index(i)] = roll(value, VEL[i][1], 0)[:ny]

    lane = lanes((ny, nz))
    for x in range(nx):
        fluid = solid[x] == 0
        for k in range(2):
            for i in range(19):
                cx, cy, cz = VEL[i]
                source = x - cx
                if cy:
                    value = roll(post_ref[k, i, source + 1], cy, 0)[:ny]
                else:
                    value = post_ref[k, i, source + 1, 0:ny]
                if cz == 1:
                    edge = roll(edge_ref[k, 0, ZP.index(i)], -(source + 2), 1)
                    value = jnp.where(lane == 0, edge, roll(value, 1, 1))
                elif cz == -1:
                    edge = roll(edge_ref[k, 1, ZM.index(i)], nz - 1 - (source + 2), 1)
                    value = jnp.where(lane == nz - 1, edge, roll(value, -1, 1))
                if i:
                    value = jnp.where(value < LIMIT, value, post_ref[k, OPP[i], x + 1, 0:ny])
                out[k, i, x] = jnp.where(fluid, value, pop[k, i, x])


def swap(value, axis, count, first):
    pairs = [(i, (i + 1 if i % 2 == first else i - 1) % count) for i in range(count)]
    return lax.ppermute(value, axis, pairs)


def call(kernel, name, out_shape, *args, scratch=(), flops=200000):
    vmem = pl.BlockSpec(memory_space=pltpu.VMEM)
    return pl.pallas_call(
        kernel,
        name=name,
        out_shape=[jax.ShapeDtypeStruct(s, jnp.float32) for s in out_shape],
        in_specs=[vmem] * len(args),
        out_specs=[vmem] * len(out_shape),
        scratch_shapes=[pltpu.VMEM(s, jnp.float32) for s in scratch],
        compiler_params=pltpu.CompilerParams(vmem_limit_bytes=24 * 2**20),
        cost_estimate=pl.CostEstimate(flops=flops, bytes_accessed=flops, transcendentals=0),
    )(*args)


def body(sizes, pop, solid):
    nx, ny, nz = solid.shape
    count = y_index(nx)[-1]
    wide = nx + 4
    face = (HALO, ny, nz)
    field, send_a, send_b, rows, sheets = call(
        first_kernel, "local", [(5, nx, ny, nz), face, face, (count, 8, nz), (2, ny, nz)], pop, solid
    )
    from_a, from_b = swap(send_a, "gx", sizes["gx"], 0), swap(send_b, "gx", sizes["gx"], 1)
    (rows,) = call(functools.partial(y_kernel, nx), "rows", [(count, 8, nz)], rows, from_a, from_b)
    from_y = [swap(rows, "gy", sizes["gy"], 0)]
    if sizes["gy"] > 2:
        from_y.append(swap(rows, "gy", sizes["gy"], 1))
    y_parts = len(from_y)
    tall = (ny + 8, nz)
    own_a, own_b = call(
        functools.partial(z_kernel, nx, y_parts), "sheets", [tall, tall], sheets, from_a, from_b, *from_y
    )
    zf_b, zf_a = swap(own_b, "gz", sizes["gz"], 1), swap(own_a, "gz", sizes["gz"], 0)
    scratch = [(2, wide) + tall] * 3 + [(2, nx + 2) + tall] * 2 + [(2, 19, nx + 2) + tall, (2, 2, 5, ny, nz)]
    (result,) = call(
        functools.partial(last_kernel, nx, y_parts),
        "finish",
        [pop.shape],
        pop, solid, field, from_a, from_b, own_a, own_b, zf_a, zf_b, *from_y,
        scratch=scratch,
    )
    return result


def solution(mesh):
    sizes = dict(mesh.shape)
    assert all(n % 2 == 0 for n in sizes.values())
    spec = P(None, None, "gx", "gy", "gz")
    step = functools.partial(body, sizes)
    return jax.shard_map(step, mesh=mesh, in_specs=(spec, P("gx", "gy", "gz")), out_specs=spec, check_vma=False)
```

time: 80.7 us -> 23.2 us (0.29)
  local copies, waits for them, and re-layouts: 21.3 us -> 2.05 us
  waiting for transfers between devices: 27.9 us -> 9.19 us
  other arithmetic: 12.5 us -> 0 us
  starting transfers between devices: 14.3 us -> 8.71 us
  matrix products: 3.77 us -> 0 us
  Pallas kernels: 0 us -> 3 us
    ppermute x12 -> x5, waiting for transfers between devices: 27.9 us -> 9.19 us  [swap(): return lax.ppermute(value, axis, pairs)]
    slice x9 -> x0, local copies, waits for them, and re-layouts: 10.4 us -> none  [the longest x5 6.56 us: extended(): lax.slice_in_dim(block, block.shape[dim] - width, None, axis=dim)]
    ppermute x2 -> x0, local copies, waits for them, and re-layouts: 7.36 us -> none  [the longest x1 4.15 us: extended(): lax.ppermute(lax.slice_in_dim(block, 0, width, axis=dim), axis, backward)]
    concatenate x3 -> x0, other arithmetic: 6.5 us -> none  [extended(): block = jnp.concatenate([low, block, high], axis=dim)]
    ppermute x12 -> x5, starting transfers between devices: 14.3 us -> 8.71 us  [swap(): return lax.ppermute(value, axis, pairs)]
    dot_general x3 -> x0, matrix products: 3.77 us -> none  [the longest x2 2.16 us: collide(): jnp.einsum('ia,axyz->ixyz', vel, velocity, precision=lax.Precision.HIGHEST)]
    pallas_call x0 -> x4, Pallas kernels: none -> 3 us  [call(): pl.pallas_call(kernel, name=name, out_shape=[jax.ShapeDtypeStruct(s, jnp....]
    reduce_sum x2 -> x0, other arithmetic: 1.67 us -> none  [the longest x1 1.37 us: body(): rho = jnp.sum(populations, axis=1)]
  transfers between devices with their start and end apart: 12 -> 5, of which waited for: 10 -> 4; matrix products, arithmetic and copies ran while one was open for 8% -> 0% of each run, Pallas kernels for 0% -> 0%
where the time goes in v1:
time: 23.2 us; the launch traced here: 23 us
  waiting for transfers between devices  9.19 us (40%)
  starting transfers between devices  8.71 us (38%)
  Pallas kernels  3 us (13%)
  local copies, waits for them, and re-layouts  2.05 us (9%)
    ppermute x5, waiting for transfers between devices, swap(): return lax.ppermute(value, axis, pairs)  9.19 us
    ppermute x5, starting transfers between devices, swap(): return lax.ppermute(value, axis, pairs)  8.71 us
    pallas_call x4, Pallas kernels, call(): pl.pallas_call(kernel, name=name, out_shape=[jax.ShapeDtypeStruct(s, jnp....  3 us
    unnamed x6, local copies, waits for them, and re-layouts  2.05 us
  transfers between devices with their start and end apart: 5, of which 4 were waited for; matrix products, arithmetic and copies ran while one was open for 0% of the time, Pallas kernels for 0%

profile of v1, /device:TPU:0, one launch (start us, length us, event | category | flops | bytes accessed | tf_op | source)
XLA Modules:
  0.0 23.0 jit_solution(6069948004598123900)
XLA Ops:
  0.0 0.0 copy-start
  0.0 1.3 %copy-done = f32[2,19,4,16,128]{4,3,2,1,0:T(8,128)S(1)} copy-done((f32[2,19,4,16,128]{4,3,2,1,0:T(8,128)S(1)}, f32[2,19,4,16,128]{4,3,2,1,0:T(8,128)}, u32[]{:S(2)}) %copy-start) | copy-done | bytes 1245208
  1.3 0.0 copy-start.2
  1.3 0.8 %copy-done.2 = s32[4,16,128]{2,1,0:T(8,128)S(1)} copy-done((s32[4,16,128]{2,1,0:T(8,128)S(1)}, s32[4,16,128]{2,1,0:T(8,128)}, u32[]{:S(2)}) %copy-start.2) | copy-done | bytes 32792
  2.1 0.0 copy-start.1
  2.1 0.3 %local.1 = (f32[5,4,16,128]{3,2,1,0:T(8,128)S(1)}, f32[12,16,128]{2,1,0:T(8,128)S(1)}, f32[12,16,128]{2,1,0:T(8,128)S(1)}, f32[56,8,128]{2,1,0:T(8,128)S(1)}, f32[2,16,128]{2,1,0:T(8,128)S(1)}) custom-call(f32[2,19,4,16,128]{4,3,2,1,0:T(8,128)S(1)} %copy-done, s32[4,16,128]{2,1,0:T(8,128)S(1)} %copy-done.2), custom_call_target="tpu_custom_call" | custom-call | flops 200000 | bytes 200000 | tf_op jit(solution)/shard_map/local/pallas_call | solution.py:354
  2.4 3.0 %collective-permute-start = (f32[12,16,128]{2,1,0:T(8,128)S(1)}, f32[12,16,128]{2,1,0:T(8,128)S(1)}, u32[]{:S(2)}, u32[]{:S(2)}) collective-permute-start(f32[12,16,128]{2,1,0:T(8,128)S(1)} %get-tuple-element.13), channel_id=1, source_target_pairs={{0,8},{8,0},{16,24},{24,16},{1,9},{9,1},{17,25},{25,17},{2,10},{10... | collective-permute-start | bytes 294920 | tf_op jit(solution)/shard_map/ppermute | solution.py:349
  5.4 1.5 %collective-permute-start.1 = (f32[12,16,128]{2,1,0:T(8,128)S(1)}, f32[12,16,128]{2,1,0:T(8,128)S(1)}, u32[]{:S(2)}, u32[]{:S(2)}) collective-permute-start(f32[12,16,128]{2,1,0:T(8,128)S(1)} %get-tuple-element.14), channel_id=1, source_target_pairs={{0,24},{8,16},{16,8},{24,0},{1,25},{9,17},{17,9},{25,1},{2,26},{10... | collective-permute-start | bytes 294920 | tf_op jit(solution)/shard_map/ppermute | solution.py:349
  6.9 1.6 %collective-permute-done.from_a = f32[12,16,128]{2,1,0:T(8,128)S(1)} collective-permute-done((f32[12,16,128]{2,1,0:T(8,128)S(1)}, f32[12,16,128]{2,1,0:T(8,128)S(1)}, u32[]{:S(2)}, u32[]{:S(2)}) %collective-permute-start) | collective-permute-done | bytes 98336 | tf_op jit(solution)/shard_map/ppermute | solution.py:349
  8.5 3.1 %collective-permute-done.1.from_b = f32[12,16,128]{2,1,0:T(8,128)S(1)} collective-permute-done((f32[12,16,128]{2,1,0:T(8,128)S(1)}, f32[12,16,128]{2,1,0:T(8,128)S(1)}, u32[]{:S(2)}, u32[]{:S(2)}) %collective-permute-start.1) | collective-permute-done | bytes 98336 | tf_op jit(solution)/shard_map/ppermute | solution.py:349
  11.6 0.1 collective-permute-start.2
  11.7 1.5 %collective-permute-done.2.rest_0_ = f32[56,8,128]{2,1,0:T(8,128)S(1)} collective-permute-done((f32[56,8,128]{2,1,0:T(8,128)S(1)}, f32[56,8,128]{2,1,0:T(8,128)S(1)}, u32[]{:S(2)}, u32[]{:S(2)}) %collective-permute-start.2) | collective-permute-done | bytes 229408 | tf_op jit(solution)/shard_map/ppermute | solution.py:349
  13.2 0.3 %sheets.1 = (f32[24,128]{1,0:T(8,128)S(1)}, f32[24,128]{1,0:T(8,128)S(1)}) custom-call(f32[2,16,128]{2,1,0:T(8,128)S(1)} %get-tuple-element.15.sheets, f32[12,16,128]{2,1,0:T(8,128)S(1)} %collective-permute-done.from_a, f32[12,16,128]{2,1,0:T(8,128)S(1)} %collective-permute-done.1.from_b, f32[56,8,128]{2,1,0:T(8,128)S(1)} %collective-permute-done.2.rest_0_), custom_call_target="tpu_custom_call" | custom-call | flops 200000 | bytes 200000 | tf_op jit(solution)/shard_map/sheets/pallas_call | solution.py:354
  13.5 1.6 %collective-permute-start.3 = (f32[24,128]{1,0:T(8,128)S(1)}, f32[24,128]{1,0:T(8,128)S(1)}, u32[]{:S(2)}, u32[]{:S(2)}) collective-permute-start(f32[24,128]{1,0:T(8,128)S(1)} %get-tuple-element.17.own_a), channel_id=1, source_target_pairs={{0,1},{1,0},{2,3},{3,2},{4,5},{5,4},{6,7},{7,6},{8,9},{9,8},{10,11... | collective-permute-start | bytes 36872 | tf_op jit(solution)/shard_map/ppermute | solution.py:349
  15.1 2.5 %collective-permute-start.4 = (f32[24,128]{1,0:T(8,128)S(1)}, f32[24,128]{1,0:T(8,128)S(1)}, u32[]{:S(2)}, u32[]{:S(2)}) collective-permute-start(f32[24,128]{1,0:T(8,128)S(1)} %get-tuple-element.18.own_b), channel_id=1, source_target_pairs={{0,3},{1,2},{2,1},{3,0},{4,7},{5,6},{6,5},{7,4},{8,11},{9,10},{10,... | collective-permute-start | bytes 36872 | tf_op jit(solution)/shard_map/ppermute | solution.py:349
  17.6 0.0 collective-permute-done.3.zf_a
  17.6 3.0 %collective-permute-done.4.zf_b = f32[24,128]{1,0:T(8,128)S(1)} collective-permute-done((f32[24,128]{1,0:T(8,128)S(1)}, f32[24,128]{1,0:T(8,128)S(1)}, u32[]{:S(2)}, u32[]{:S(2)}) %collective-permute-start.4) | collective-permute-done | bytes 12320 | tf_op jit(solution)/shard_map/ppermute | solution.py:349
  20.6 0.0 copy-done.1
  20.6 2.3 %finish.1 = f32[2,19,4,16,128]{4,3,2,1,0:T(8,128)} custom-call(f32[2,19,4,16,128]{4,3,2,1,0:T(8,128)S(1)} %copy-done.1, s32[4,16,128]{2,1,0:T(8,128)S(1)} %copy-done.2, f32[5,4,16,128]{3,2,1,0:T(8,128)S(1)} %get-tuple-element.12.field, f32[12,16,128]{2,1,0:T(8,128)S(1)} %collective-permute-done.from_a, f32[12,16,128]{2,1,0:T(8,128)S(1)} %collective-permute-done.1.from_b, ...), custom_call_target="tpu_custom_call" | custom-call | flops 200000 | bytes 200000 | tf_op jit(solution)/shard_map/finish/pallas_call | solution.py:354
  (1 shorter events, 0.0 us)
Async XLA Ops:
  0.0 1.3 %copy-start = (f32[2,19,4,16,128]{4,3,2,1,0:T(8,128)S(1)}, f32[2,19,4,16,128]{4,3,2,1,0:T(8,128)}, u32[]{:S(2)}) copy-start(f32[2,19,4,16,128]{4,3,2,1,0:T(8,128)} %pop.3) | copy-start | bytes 3735556
  1.3 0.8 %copy-start.2 = (s32[4,16,128]{2,1,0:T(8,128)S(1)}, s32[4,16,128]{2,1,0:T(8,128)}, u32[]{:S(2)}) copy-start(s32[4,16,128]{2,1,0:T(8,128)} %solid.3) | copy-start | bytes 98308
  2.1 18.6 %copy-start.1 = (f32[2,19,4,16,128]{4,3,2,1,0:T(8,128)S(1)}, f32[2,19,4,16,128]{4,3,2,1,0:T(8,128)}, u32[]{:S(2)}) copy-start(f32[2,19,4,16,128]{4,3,2,1,0:T(8,128)} %pop.3) | copy-start | bytes 3735556
  2.4 6.1 %collective-permute-start = (f32[12,16,128]{2,1,0:T(8,128)S(1)}, f32[12,16,128]{2,1,0:T(8,128)S(1)}, u32[]{:S(2)}, u32[]{:S(2)}) collective-permute-start(f32[12,16,128]{2,1,0:T(8,128)S(1)} %get-tuple-element.13), channel_id=1, source_target_pairs={{0,8},{8,0},{16,24},{24,16},{1,9},{9,1},{17,25},{25,17},{2,10},{10... | collective-permute-start | bytes 294920 | tf_op jit(solution)/shard_map/ppermute | solution.py:349
  5.4 6.2 %collective-permute-start.1 = (f32[12,16,128]{2,1,0:T(8,128)S(1)}, f32[12,16,128]{2,1,0:T(8,128)S(1)}, u32[]{:S(2)}, u32[]{:S(2)}) collective-permute-start(f32[12,16,128]{2,1,0:T(8,128)S(1)} %get-tuple-element.14), channel_id=1, source_target_pairs={{0,24},{8,16},{16,8},{24,0},{1,25},{9,17},{17,9},{25,1},{2,26},{10... | collective-permute-start | bytes 294920 | tf_op jit(solution)/shard_map/ppermute | solution.py:349
  11.6 1.6 %collective-permute-start.2 = (f32[56,8,128]{2,1,0:T(8,128)S(1)}, f32[56,8,128]{2,1,0:T(8,128)S(1)}, u32[]{:S(2)}, u32[]{:S(2)}) collective-permute-start(f32[56,8,128]{2,1,0:T(8,128)S(1)} %rows.1), channel_id=1, source_target_pairs={{0,4},{4,0},{1,5},{5,1},{2,6},{6,2},{3,7},{7,3},{8,12},{12,8},{9,1... | collective-permute-start | bytes 688136 | tf_op jit(solution)/shard_map/ppermute | solution.py:349
  13.5 4.1 %collective-permute-start.3 = (f32[24,128]{1,0:T(8,128)S(1)}, f32[24,128]{1,0:T(8,128)S(1)}, u32[]{:S(2)}, u32[]{:S(2)}) collective-permute-start(f32[24,128]{1,0:T(8,128)S(1)} %get-tuple-element.17.own_a), channel_id=1, source_target_pairs={{0,1},{1,0},{2,3},{3,2},{4,5},{5,4},{6,7},{7,6},{8,9},{9,8},{10,11... | collective-permute-start | bytes 36872 | tf_op jit(solution)/shard_map/ppermute | solution.py:349
  15.1 5.5 %collective-permute-start.4 = (f32[24,128]{1,0:T(8,128)S(1)}, f32[24,128]{1,0:T(8,128)S(1)}, u32[]{:S(2)}, u32[]{:S(2)}) collective-permute-start(f32[24,128]{1,0:T(8,128)S(1)} %get-tuple-element.18.own_b), channel_id=1, source_target_pairs={{0,3},{1,2},{2,1},{3,0},{4,7},{5,6},{6,5},{7,4},{8,11},{9,10},{10,... | collective-permute-start | bytes 36872 | tf_op jit(solution)/shard_map/ppermute | solution.py:349

commit v2 on v1

v2 whole, which is shorter than its diff:
```python
import functools

import jax
import jax.numpy as jnp
from jax import lax
from jax.experimental import pallas as pl
from jax.experimental.pallas import tpu as pltpu
from jax.sharding import PartitionSpec as P


VEL = [
    (0, 0, 0),
    (1, 0, 0), (-1, 0, 0), (0, 1, 0), (0, -1, 0), (0, 0, 1), (0, 0, -1),
    (1, 1, 0), (-1, -1, 0), (1, -1, 0), (-1, 1, 0),
    (1, 0, 1), (-1, 0, -1), (1, 0, -1), (-1, 0, 1),
    (0, 1, 1), (0, -1, -1), (0, 1, -1), (0, -1, 1),
]
WEIGHT = [1.0 / 3.0] + [1.0 / 18.0] * 6 + [1.0 / 36.0] * 12
OPP = [0, 2, 1, 4, 3, 6, 5, 8, 7, 10, 9, 12, 11, 14, 13, 16, 15, 18, 17]
COUPLING = 0.9
TAU = (1.0, 0.8)
WALL = (0.3, 1.5)
W1, W2 = 1.0 / 18.0, 1.0 / 36.0
BLOCKED = 1e30
LIMIT = 1e29

XP = [i for i in range(19) if VEL[i][0] == 1]
XM = [i for i in range(19) if VEL[i][0] == -1]
ZP = [i for i in range(19) if VEL[i][2] == 1]
ZM = [i for i in range(19) if VEL[i][2] == -1]
YP = [i for i in range(19) if VEL[i][1] == 1]
YPAIR = [(i, VEL.index((VEL[i][0], -1, VEL[i][2]))) for i in YP]
HALO = 12


def lanes(shape):
    return lax.broadcasted_iota(jnp.int32, shape, len(shape) - 1)


def roll(v, shift, axis):
    shift = shift % v.shape[axis]
    return pltpu.roll(v, shift, axis) if shift else v


def up(v):
    return roll(v, -1, 0)


def down(v):
    return roll(v, 1, 0)


def fold(v, rows):
    tile = lax.broadcasted_iota(jnp.int32, (8, v.shape[1]), 0)
    return jnp.where(tile < 4, v[:8], v[rows - 8 : rows])


def parity(axis):
    return lax.rem(lax.axis_index(axis), 2) == 0


def put(sheet, value, source, target):
    return jnp.where(lanes(sheet.shape) == target, roll(value, target - source, 1), sheet)


def y_index(nx):
    wide, mid = nx + 4, nx + 2
    psi = lambda k, x: k * wide + x + 2
    com = lambda a, x: 2 * wide + a * mid + x + 1
    base = 2 * wide + 3 * mid
    pair = lambda j, x: base + j * nx + x
    low, high = base + 5 * nx, base + 5 * nx + 1
    return psi, com, pair, low, high, high + 1


def first_kernel(pop_hbm, solid_hbm, field, face_a, face_b, rim_a, rim_b, pop, solid, sems):
    nx, ny, nz = solid_hbm.shape
    wide = nx + 4
    flag_copy = pltpu.make_async_copy(solid_hbm, solid, sems.at[nx])
    copies = [pltpu.make_async_copy(pop_hbm.at[:, :, x], pop.at[:, :, x], sems.at[x]) for x in range(nx)]
    flag_copy.start()
    for x in range(nx):
        copies[x].start()
    flag_copy.wait()
    for x in range(nx):
        copies[x].wait()
        fluid = solid[x] == 0
        q = []
        rho0 = rho1 = None
        for i in range(19):
            p0, p1 = pop[0, i, x], pop[1, i, x]
            rho0 = p0 if rho0 is None else rho0 + p0
            rho1 = p1 if rho1 is None else rho1 + p1
            q.append(p0 * (1.0 / TAU[0]) + p1 * (1.0 / TAU[1]))
        inverse = 1.0 / (rho0 * (1.0 / TAU[0]) + rho1 * (1.0 / TAU[1]))
        field[0, x] = jnp.where(fluid, rho0, -WALL[0])
        field[1, x] = jnp.where(fluid, rho1, -WALL[1])
        for a in range(3):
            total = None
            for i in range(1, 19):
                if VEL[i][a] == 1:
                    term = q[i] - q[OPP[i]]
                    total = term if total is None else total + term
            field[2 + a, x] = total * inverse
    even = parity("gx")
    faces, rims = [], []
    for step, dirs, edge, inner in ((1, XP, nx - 1, nx - 2), (-1, XM, 0, 1)):
        face = [field[f, edge] for f in range(5)] + [pop[1, i, edge] for i in dirs] + [field[f, inner] for f in range(2)]
        rim = jnp.zeros((ny, nz), jnp.float32)
        for cz, z_dirs, z_edge, z_inner in ((1, ZP, nz - 1, nz - 2), (-1, ZM, 0, 1)):
            near, far = rim_lanes(wide, step, cz)
            for k in range(2):
                for f, lane in ((k, z_edge), (10 + k, z_inner)):
                    rim = put(rim, face[k], lane, f * wide + near)
                    rim = put(rim, face[10 + k], lane, f * wide + far)
            for a in range(3):
                rim = put(rim, face[2 + a], z_edge, (2 + a) * wide + near)
            i = VEL.index((step, 0, cz))
            rim = put(rim, face[5 + dirs.index(i)], z_edge, (5 + z_dirs.index(i)) * wide + near)
        faces.append(face)
        rims.append(rim)
    for f in range(HALO):
        face_a[f] = jnp.where(even, faces[0][f], faces[1][f])
        face_b[f] = jnp.where(even, faces[1][f], faces[0][f])
    rim_a[...] = jnp.where(even, rims[0], rims[1])
    rim_b[...] = jnp.where(even, rims[1], rims[0])


def rim_lanes(wide, step, cz):
    if step == 1:
        return (1, 0) if cz == 1 else (3, 2)
    return (wide - 2, wide - 1) if cz == 1 else (wide - 4, wide - 3)


def column_kernel(field, pop, sheets):
    nx, ny, nz = field.shape[1:]
    wide = nx + 4
    for side, edge, inner, dirs in ((0, nz - 1, nz - 2, ZP), (1, 0, 1, ZM)):
        sheet = jnp.zeros((ny, nz), jnp.float32)
        for x in range(nx):
            for f in range(5):
                sheet = put(sheet, field[f, x], edge, f * wide + x + 2)
            for j, i in enumerate(dirs):
                sheet = put(sheet, pop[1, i, x], edge, (5 + j) * wide + x + 2)
            for k in range(2):
                sheet = put(sheet, field[k, x], inner, (10 + k) * wide + x + 2)
        sheets[side] = sheet


def join_kernel(nx, sheets, from_a, from_b, joined, rows_out):
    ny = from_a.shape[0]
    wide = nx + 4
    even = parity("gx")
    a, b = from_a[...], from_b[...]
    above, below = jnp.where(even, a, b), jnp.where(even, b, a)
    place = lax.rem(lanes(a.shape), wide)
    for side, shift in ((0, 0), (1, 2)):
        sheet = jnp.where(place < 2, roll(below, -shift, 1), sheets[side])
        sheet = jnp.where(place >= nx + 2, roll(above, shift, 1), sheet)
        joined[side] = sheet
        rows_out[side] = fold(sheet, ny)


def sides(even, from_a, from_b, f):
    a, b = from_a[f], from_b[f]
    return jnp.where(even, a, b), jnp.where(even, b, a)


def y_kernel(nx, field, pop, from_a, from_b, rows_out):
    psi, com, pair, low, high, _ = y_index(nx)
    ny, nz = from_a.shape[1:]
    even = parity("gx")
    tile = lax.broadcasted_iota(jnp.int32, (8, nz), 0)
    for k in range(2):
        for x in range(nx):
            rows_out[psi(k, x)] = fold(field[k, x], ny)
        above, below = sides(even, from_a, from_b, k)
        rows_out[psi(k, nx)], rows_out[psi(k, -1)] = fold(above, ny), fold(below, ny)
        above, below = sides(even, from_a, from_b, 10 + k)
        rows_out[psi(k, nx + 1)], rows_out[psi(k, -2)] = fold(above, ny), fold(below, ny)
    for a in range(3):
        for x in range(nx):
            rows_out[com(a, x)] = fold(field[2 + a, x], ny)
        above, below = sides(even, from_a, from_b, 2 + a)
        rows_out[com(a, nx)], rows_out[com(a, -1)] = fold(above, ny), fold(below, ny)
    for j, (plus, minus) in enumerate(YPAIR):
        for x in range(nx):
            rows_out[pair(j, x)] = jnp.where(tile < 4, pop[1, minus, x, 0:8], pop[1, plus, x, ny - 8 : ny])
    for where, step, dirs in ((low, 1, XP), (high, -1, XM)):
        plus, minus = dirs.index(VEL.index((step, 1, 0))) + 5, dirs.index(VEL.index((step, -1, 0))) + 5
        take = 1 if step == 1 else 0
        top, bottom = sides(even, from_a, from_b, minus)[take], sides(even, from_a, from_b, plus)[take]
        rows_out[where] = jnp.where(tile < 4, top[:8], bottom[ny - 8 :])


def merge_rows(y_even, from_y, n):
    if len(from_y) == 1:
        return from_y[0][n]
    a, b = from_y[0][n], from_y[1][n]
    tile = lax.broadcasted_iota(jnp.int32, a.shape, 0)
    return jnp.where((tile < 4) == y_even, a, b)


def z_kernel(y_parts, joined, *rest):
    from_y, (send_a, send_b) = rest[:y_parts], rest[y_parts:]
    y_even, z_even = parity("gy"), parity("gz")
    made = [jnp.concatenate([joined[side], merge_rows(y_even, from_y, side)], axis=0) for side in range(2)]
    send_a[...] = jnp.where(z_even, made[0], made[1])
    send_b[...] = jnp.where(z_even, made[1], made[0])


def posts(rho, vel, fluid, dirs, pop):
    out = {}
    for k in range(2):
        u = vel[k]
        base = rho[k] * (1.0 - 1.5 * (u[0] * u[0] + u[1] * u[1] + u[2] * u[2]))
        for i in dirs:
            rows = pop(k, i, True)
            cut = (lambda v: v[:rows]) if rows != rho[k].shape[0] else (lambda v: v)
            if i == 0:
                equil = base * WEIGHT[0]
            else:
                lead = next(a for a in range(3) if VEL[i][a])
                main = i if VEL[i][lead] == 1 else OPP[i]
                along = None
                for a in range(3):
                    c = VEL[main][a]
                    if c:
                        along = u[a] if along is None else (along + u[a] if c == 1 else along - u[a])
                flow = rho[k] * along
                even = base * WEIGHT[i] + (4.5 * WEIGHT[i]) * (flow * along)
                odd = (3.0 * WEIGHT[i]) * flow
                equil = even + odd if main == i else even - odd
            equil = cut(equil)
            if k == 0:
                post = equil
            else:
                post = (1.0 / TAU[1]) * equil + (1.0 - 1.0 / TAU[1]) * pop(k, i, False)
            out[k, i] = jnp.where(cut(fluid), post, BLOCKED)
    return out


def last_kernel(nx, y_parts, pop, solid, field, from_a, from_b, own_a, own_b, zf_a, zf_b, *rest):
    from_y, (out_hbm, out, t_ref, dy_ref, dz_ref, gy_ref, gz_ref, post_ref, edge_ref, sems) = rest[:y_parts], rest[y_parts:]
    psi, com, pair, low, high, _ = y_index(nx)
    wide = nx + 4
    ny, nz = from_a.shape[1:]
    x_even, y_even, z_even = parity("gx"), parity("gy"), parity("gz")
    rows = lambda n: merge_rows(y_even, from_y, n)
    above = lambda f: sides(x_even, from_a, from_b, f)[0]
    below = lambda f: sides(x_even, from_a, from_b, f)[1]
    own_hi, own_lo = jnp.where(z_even, own_a[...], own_b[...]), jnp.where(z_even, own_b[...], own_a[...])
    z_hi, z_lo = jnp.where(z_even, zf_a[...], zf_b[...]), jnp.where(z_even, zf_b[...], zf_a[...])
    tall = (ny + 8, nz)

    def signed(k, x):
        if x < 0:
            main = below(k if x == -1 else 10 + k)
        elif x >= nx:
            main = above(k if x == nx else 10 + k)
        else:
            main = field[k, x]
        return jnp.concatenate([main, rows(psi(k, x))], axis=0)

    lane = lanes(tall)
    for k in range(2):
        for x in range(-2, nx + 2):
            a = jnp.abs(signed(k, x))
            column = k * wide + x + 2
            minus = jnp.where(lane == 0, jnp.abs(roll(z_lo, -column, 1)), roll(a, 1, 1))
            plus = jnp.where(lane == nz - 1, jnp.abs(roll(z_hi, nz - 1 - column, 1)), roll(a, -1, 1))
            a_up, a_down = up(a), down(a)
            z_sum, dz, dy = plus + minus, plus - minus, a_up - a_down
            t_ref[k, x + 2] = W1 * a + W2 * (a_up + a_down + z_sum)
            dy_ref[k, x + 2] = dy
            dz_ref[k, x + 2] = dz
            if -2 < x < nx + 1:
                gy_ref[k, x + 1] = W1 * dy + W2 * (up(z_sum) - down(z_sum))
                gz_ref[k, x + 1] = W1 * dz + W2 * (up(dz) + down(dz))

    for side, sheet, own, dirs in ((0, z_lo, own_lo, ZP), (1, z_hi, own_hi, ZM)):
        part = lambda s, f: roll(s, -f * wide, 1)
        gradient, sign = [], [part(sheet, 0), part(sheet, 1)]
        for k in range(2):
            a, beyond, inside = jnp.abs(sign[k]), jnp.abs(part(sheet, 10 + k)), jnp.abs(part(own, k))
            plus, minus = (inside, beyond) if side == 0 else (beyond, inside)
            a_up, a_down = up(a), down(a)
            z_sum, dz, dy = plus + minus, plus - minus, a_up - a_down
            t = W1 * a + W2 * (a_up + a_down + z_sum)
            right, left = (lambda v: roll(v, -1, 1)), (lambda v: roll(v, 1, 1))
            gradient.append((
                right(t) - left(t),
                W1 * dy + W2 * (up(z_sum) - down(z_sum) + right(dy) + left(dy)),
                W1 * dz + W2 * (up(dz) + down(dz) + right(dz) + left(dz)),
            ))
        common = [part(sheet, 2 + a) for a in range(3)]
        vel = [[common[a] - (COUPLING * TAU[k]) * gradient[1 - k][a] for a in range(3)] for k in range(2)]
        rho = (jnp.abs(sign[0]), jnp.abs(sign[1]))
        population = lambda k, i, ask: ny + 8 if ask else part(sheet, 5 + dirs.index(i))
        for (k, i), value in posts(rho, vel, sign[0] > 0.0, dirs, population).items():
            edge_ref[k, side, dirs.index(i)] = roll(value, VEL[i][1], 0)[:ny]

    lane_of = lanes((ny, nz))

    def finish(x):
        fluid = solid[x] == 0
        for k in range(2):
            for i in range(19):
                cx, cy, cz = VEL[i]
                source = x - cx
                if cy:
                    value = roll(post_ref[k, i, source + 1], cy, 0)[:ny]
                else:
                    value = post_ref[k, i, source + 1, 0:ny]
                if cz == 1:
                    edge = roll(edge_ref[k, 0, ZP.index(i)], -(source + 2), 1)
                    value = jnp.where(lane_of == 0, edge, roll(value, 1, 1))
                elif cz == -1:
                    edge = roll(edge_ref[k, 1, ZM.index(i)], nz - 1 - (source + 2), 1)
                    value = jnp.where(lane_of == nz - 1, edge, roll(value, -1, 1))
                if i:
                    value = jnp.where(value < LIMIT, value, post_ref[k, OPP[i], x + 1, 0:ny])
                out[k, i, x] = jnp.where(fluid, value, pop[k, i, x])
            pltpu.make_async_copy(out.at[k, :, x], out_hbm.at[k, :, x], sems.at[k, x]).start()

    for x in range(-1, nx + 1):
        gradient = []
        for k in range(2):
            gradient.append((
                t_ref[k, x + 3] - t_ref[k, x + 1],
                gy_ref[k, x + 1] + W2 * (dy_ref[k, x + 3] + dy_ref[k, x + 1]),
                gz_ref[k, x + 1] + W2 * (dz_ref[k, x + 3] + dz_ref[k, x + 1]),
            ))
        common = []
        for a in range(3):
            main = below(2 + a) if x < 0 else above(2 + a) if x == nx else field[2 + a, x]
            common.append(jnp.concatenate([main, rows(com(a, x))], axis=0))
        vel = [[common[a] - (COUPLING * TAU[k]) * gradient[1 - k][a] for a in range(3)] for k in range(2)]
        s0, s1 = signed(0, x), signed(1, x)

        def population(k, i, ask, x=x):
            if ask:
                return ny + 8 if VEL[i][1] else ny
            if x < 0:
                main = below(5 + XP.index(i))
            elif x == nx:
                main = above(5 + XM.index(i))
            else:
                main = pop[1, i, x]
            if not VEL[i][1]:
                return main
            j = next(j for j, both in enumerate(YPAIR) if i in both)
            return jnp.concatenate([main, rows(low if x < 0 else high if x == nx else pair(j, x))], axis=0)

        dirs = XP if x < 0 else XM if x == nx else range(19)
        for (k, i), value in posts((jnp.abs(s0), jnp.abs(s1)), vel, s0 > 0.0, dirs, population).items():
            post_ref[k, i, x + 1, 0 : value.shape[0]] = value
        if x > 0:
            finish(x - 1)
    for x in range(nx):
        for k in range(2):
            pltpu.make_async_copy(out.at[k, :, x], out_hbm.at[k, :, x], sems.at[k, x]).wait()


def swap(value, axis, count, first):
    pairs = [(i, (i + 1 if i % 2 == first else i - 1) % count) for i in range(count)]
    return lax.ppermute(value, axis, pairs)


def call(kernel, out_shape, *args, scratch=(), hbm_in=0, hbm_out=0, flops=200000, limit=16 * 2**20):
    space = lambda n, held: [pl.BlockSpec(memory_space=pltpu.HBM if j < held else pltpu.VMEM) for j in range(n)]
    args = [pltpu.with_memory_space_constraint(v, pltpu.HBM) if j < hbm_in else v for j, v in enumerate(args)]
    return pl.pallas_call(
        kernel,
        out_shape=[jax.ShapeDtypeStruct(*(s if isinstance(s[-1], type) else (s, jnp.float32))) for s in out_shape],
        in_specs=space(len(args), hbm_in),
        out_specs=space(len(out_shape), hbm_out),
        scratch_shapes=list(scratch),
        compiler_params=pltpu.CompilerParams(vmem_limit_bytes=limit),
        cost_estimate=pl.CostEstimate(flops=flops, bytes_accessed=flops, transcendentals=0),
    )(*args)


def body(sizes, pop, solid):
    return step(sizes, pop, solid)


def step(sizes, pop, solid):
    nx, ny, nz = solid.shape
    count = y_index(nx)[-1]
    wide = nx + 4
    face, plane, tall = (HALO, ny, nz), (ny, nz), (ny + 8, nz)
    gx, gy, gz = sizes["gx"], sizes["gy"], sizes["gz"]
    y_parts = 1 if gy == 2 else 2
    field, face_a, face_b, rim_a, rim_b, pop_v, solid_v = call(
        first_kernel,
        [(5, nx, ny, nz), face, face, plane, plane, pop.shape, (solid.shape, jnp.int32)],
        pop, solid,
        scratch=[pltpu.SemaphoreType.DMA((nx + 1,))],
        hbm_in=2,
    )
    rim_b, rim_a = swap(rim_b, "gx", gx, 1), swap(rim_a, "gx", gx, 0)
    face_b, face_a = swap(face_b, "gx", gx, 1), swap(face_a, "gx", gx, 0)
    (sheets,) = call(column_kernel, [(2,) + plane], field, pop_v)
    joined, ends = call(functools.partial(join_kernel, nx), [(2,) + plane, (2, 8, nz)], sheets, rim_a, rim_b)
    ends = [swap(ends, "gy", gy, m) for m in range(y_parts)]
    own_a, own_b = call(functools.partial(z_kernel, y_parts), [tall, tall], joined, *ends)
    far_b, far_a = swap(own_b, "gz", gz, 1), swap(own_a, "gz", gz, 0)
    (rows,) = call(functools.partial(y_kernel, nx), [(count, 8, nz)], field, pop_v, face_a, face_b)
    from_y = [swap(rows, "gy", gy, m) for m in range(y_parts)]
    vmem = lambda *s: pltpu.VMEM(s, jnp.float32)
    (result,) = call(
        functools.partial(last_kernel, nx, y_parts),
        [pop.shape],
        pop_v, solid_v, field, face_a, face_b, own_a, own_b, far_a, far_b, *from_y,
        scratch=[vmem(*pop.shape)]
        + [vmem(2, wide, *tall)] * 3
        + [vmem(2, nx + 2, *tall)] * 2
        + [vmem(2, 19, nx + 2, *tall), vmem(2, 2, 5, ny, nz), pltpu.SemaphoreType.DMA((2, nx))],
        hbm_out=1,
    )
    return result


def solution(mesh):
    sizes = dict(mesh.shape)
    assert all(n % 2 == 0 for n in sizes.values())
    spec = P(None, None, "gx", "gy", "gz")
    return jax.shard_map(
        functools.partial(body, sizes),
        mesh=mesh,
        in_specs=(spec, P("gx", "gy", "gz")),
        out_specs=spec,
        check_vma=False,
    )
```

time: 23.2 us -> 27.4 us (1.18)
  waiting for transfers between devices: 9.19 us -> 12.3 us
  starting transfers between devices: 8.71 us -> 11 us
  local copies, waits for them, and re-layouts: 2.05 us -> 0 us
  Pallas kernels: 3 us -> 3.96 us
    ppermute x5 -> x8, waiting for transfers between devices: 9.19 us -> 12.3 us  [swap(): return lax.ppermute(value, axis, pairs)]
    ppermute x5 -> x8, starting transfers between devices: 8.71 us -> 11 us  [swap(): return lax.ppermute(value, axis, pairs)]
    unnamed x6 -> x0, local copies, waits for them, and re-layouts: 2.05 us -> none
    pallas_call x4 -> x6, Pallas kernels: 3 us -> 3.96 us  [call(): pl.pallas_call(kernel, out_shape=[jax.ShapeDtypeStruct(*(s if isinstance(...]
  transfers between devices with their start and end apart: 5 -> 8, of which waited for: 4 -> 6; matrix products, arithmetic and copies ran while one was open for 0% -> 0% of each run, Pallas kernels for 0% -> 1%
where the time goes in v2:
time: 27.4 us; the launch traced here: 27.3 us
  waiting for transfers between devices  12.3 us (45%)
  starting transfers between devices  11 us (40%)
  Pallas kernels  3.96 us (14%)
    ppermute x8, waiting for transfers between devices, swap(): return lax.ppermute(value, axis, pairs)  12.3 us
    ppermute x8, starting transfers between devices, swap(): return lax.ppermute(value, axis, pairs)  11 us
    pallas_call x6, Pallas kernels, call(): pl.pallas_call(kernel, out_shape=[jax.ShapeDtypeStruct(*(s if isinstance(...  3.96 us
  transfers between devices with their start and end apart: 8, of which 6 were waited for; matrix products, arithmetic and copies ran while one was open for 0% of the time, Pallas kernels for 1%

profile of v2, /device:TPU:0, one launch (start us, length us, event | category | flops | bytes accessed | tf_op | source)
XLA Modules:
  0.0 27.3 jit_solution(18230622966074452181)
XLA Ops:
  0.0 1.5 %shard_map.28 = (f32[5,4,16,128]{3,2,1,0:T(8,128)S(1)}, f32[12,16,128]{2,1,0:T(8,128)S(1)}, f32[12,16,128]{2,1,0:T(8,128)S(1)}, f32[16,128]{1,0:T(8,128)S(1)}, f...) custom-call(f32[2,19,4,16,128]{4,3,2,1,0:T(8,128)} %pop_hbm.1, ...), custom_call_target="tpu_custom_call" | custom-call | flops 200000 | bytes 200000 | tf_op jit(solution)/shard_map/pallas_call | solution.py:373
  1.5 3.0 %collective-permute-start = (f32[12,16,128]{2,1,0:T(8,128)S(1)}, f32[12,16,128]{2,1,0:T(8,128)S(1)}, u32[]{:S(2)}, u32[]{:S(2)}) collective-permute-start(f32[12,16,128]{2,1,0:T(8,128)S(1)} %get-tuple-element.19), channel_id=1, source_target_pairs={{0,8},{8,0},{16,24},{24,16},{1,9},{9,1},{17,25},{25,17},{2,10},{10... | collective-permute-start | bytes 294920 | tf_op jit(solution)/shard_map/ppermute | solution.py:367
  4.5 1.5 %collective-permute-start.1 = (f32[12,16,128]{2,1,0:T(8,128)S(1)}, f32[12,16,128]{2,1,0:T(8,128)S(1)}, u32[]{:S(2)}, u32[]{:S(2)}) collective-permute-start(f32[12,16,128]{2,1,0:T(8,128)S(1)} %get-tuple-element.20), channel_id=1, source_target_pairs={{0,24},{8,16},{16,8},{24,0},{1,25},{9,17},{17,9},{25,1},{2,26},{10... | collective-permute-start | bytes 294920 | tf_op jit(solution)/shard_map/ppermute | solution.py:367
  6.0 1.6 %collective-permute-done.from_a = f32[12,16,128]{2,1,0:T(8,128)S(1)} collective-permute-done((f32[12,16,128]{2,1,0:T(8,128)S(1)}, f32[12,16,128]{2,1,0:T(8,128)S(1)}, u32[]{:S(2)}, u32[]{:S(2)}) %collective-permute-start) | collective-permute-done | bytes 98336 | tf_op jit(solution)/shard_map/ppermute | solution.py:367
  7.7 3.1 %collective-permute-done.1.from_b = f32[12,16,128]{2,1,0:T(8,128)S(1)} collective-permute-done((f32[12,16,128]{2,1,0:T(8,128)S(1)}, f32[12,16,128]{2,1,0:T(8,128)S(1)}, u32[]{:S(2)}, u32[]{:S(2)}) %collective-permute-start.1) | collective-permute-done | bytes 98336 | tf_op jit(solution)/shard_map/ppermute | solution.py:367
  10.8 0.1 collective-permute-start.7
  10.8 1.5 %collective-permute-start.2 = (f32[16,128]{1,0:T(8,128)S(1)}, f32[16,128]{1,0:T(8,128)S(1)}, u32[]{:S(2)}, u32[]{:S(2)}) collective-permute-start(f32[16,128]{1,0:T(8,128)S(1)} %get-tuple-element.21), channel_id=1, source_target_pairs={{0,8},{8,0},{16,24},{24,16},{1,9},{9,1},{17,25},{25,17},{2,10},{10... | collective-permute-start | bytes 24584 | tf_op jit(solution)/shard_map/ppermute | solution.py:367
  12.3 0.9 %collective-permute-start.3 = (f32[16,128]{1,0:T(8,128)S(1)}, f32[16,128]{1,0:T(8,128)S(1)}, u32[]{:S(2)}, u32[]{:S(2)}) collective-permute-start(f32[16,128]{1,0:T(8,128)S(1)} %get-tuple-element.22), channel_id=1, source_target_pairs={{0,24},{8,16},{16,8},{24,0},{1,25},{9,17},{17,9},{25,1},{2,26},{10... | collective-permute-start | bytes 24584 | tf_op jit(solution)/shard_map/ppermute | solution.py:367
  13.2 0.3 shard_map.29.sheets
  13.5 1.1 %collective-permute-done.2.from_a = f32[16,128]{1,0:T(8,128)S(1)} collective-permute-done((f32[16,128]{1,0:T(8,128)S(1)}, f32[16,128]{1,0:T(8,128)S(1)}, u32[]{:S(2)}, u32[]{:S(2)}) %collective-permute-start.2) | collective-permute-done | bytes 8224 | tf_op jit(solution)/shard_map/ppermute | solution.py:367
  14.6 2.3 %collective-permute-done.3.from_b = f32[16,128]{1,0:T(8,128)S(1)} collective-permute-done((f32[16,128]{1,0:T(8,128)S(1)}, f32[16,128]{1,0:T(8,128)S(1)}, u32[]{:S(2)}, u32[]{:S(2)}) %collective-permute-start.3) | collective-permute-done | bytes 8224 | tf_op jit(solution)/shard_map/ppermute | solution.py:367
  16.9 0.1 shard_map.30
  16.9 0.0 collective-permute-start.4
  17.0 1.2 %collective-permute-done.4.rest_0_ = f32[2,8,128]{2,1,0:T(8,128)S(1)} collective-permute-done((f32[2,8,128]{2,1,0:T(8,128)S(1)}, f32[2,8,128]{2,1,0:T(8,128)S(1)}, u32[]{:S(2)}, u32[]{:S(2)}) %collective-permute-start.4) | collective-permute-done | bytes 8224 | tf_op jit(solution)/shard_map/ppermute | solution.py:367
  18.1 1.6 %collective-permute-start.5 = (f32[24,128]{1,0:T(8,128)S(1)}, f32[24,128]{1,0:T(8,128)S(1)}, u32[]{:S(2)}, u32[]{:S(2)}) collective-permute-start(f32[24,128]{1,0:T(8,128)S(1)} %get-tuple-element.25.own_a), channel_id=1, source_target_pairs={{0,1},{1,0},{2,3},{3,2},{4,5},{5,4},{6,7},{7,6},{8,9},{9,8},{10,11... | collective-permute-start | bytes 36872 | tf_op jit(solution)/shard_map/ppermute | solution.py:367
  19.7 2.5 %collective-permute-start.6 = (f32[24,128]{1,0:T(8,128)S(1)}, f32[24,128]{1,0:T(8,128)S(1)}, u32[]{:S(2)}, u32[]{:S(2)}) collective-permute-start(f32[24,128]{1,0:T(8,128)S(1)} %get-tuple-element.26.own_b), channel_id=1, source_target_pairs={{0,3},{1,2},{2,1},{3,0},{4,7},{5,6},{6,5},{7,4},{8,11},{9,10},{10,... | collective-permute-start | bytes 36872 | tf_op jit(solution)/shard_map/ppermute | solution.py:367
  22.2 0.0 collective-permute-done.5.zf_a
  22.2 3.0 %collective-permute-done.6.zf_b = f32[24,128]{1,0:T(8,128)S(1)} collective-permute-done((f32[24,128]{1,0:T(8,128)S(1)}, f32[24,128]{1,0:T(8,128)S(1)}, u32[]{:S(2)}, u32[]{:S(2)}) %collective-permute-start.6) | collective-permute-done | bytes 12320 | tf_op jit(solution)/shard_map/ppermute | solution.py:367
  25.2 0.0 collective-permute-done.7.rest_0_
  25.2 2.1 %shard_map.33 = f32[2,19,4,16,128]{4,3,2,1,0:T(8,128)} custom-call(f32[2,19,4,16,128]{4,3,2,1,0:T(8,128)S(1)} %get-tuple-element.16.pop, s32[4,16,128]{2,1,0:T(8,128)S(1)} %get-tuple-element.17.solid, f32[5,4,16,128]{3,2,1,0:T(8,128)S(1)} %get-tuple-element.18.field, f32[12,16,128]{2,1,0:T(8,128)S(1)} %collective-permute-done.from_a, ...), custom_call_target="tpu_custom_call" | custom-call | flops 200000 | bytes 200000 | tf_op jit(solution)/shard_map/pallas_call | solution.py:373
  (2 shorter events, 0.0 us)
Async XLA Ops:
  1.5 6.1 %collective-permute-start = (f32[12,16,128]{2,1,0:T(8,128)S(1)}, f32[12,16,128]{2,1,0:T(8,128)S(1)}, u32[]{:S(2)}, u32[]{:S(2)}) collective-permute-start(f32[12,16,128]{2,1,0:T(8,128)S(1)} %get-tuple-element.19), channel_id=1, source_target_pairs={{0,8},{8,0},{16,24},{24,16},{1,9},{9,1},{17,25},{25,17},{2,10},{10... | collective-permute-start | bytes 294920 | tf_op jit(solution)/shard_map/ppermute | solution.py:367
  4.5 6.2 %collective-permute-start.1 = (f32[12,16,128]{2,1,0:T(8,128)S(1)}, f32[12,16,128]{2,1,0:T(8,128)S(1)}, u32[]{:S(2)}, u32[]{:S(2)}) collective-permute-start(f32[12,16,128]{2,1,0:T(8,128)S(1)} %get-tuple-element.20), channel_id=1, source_target_pairs={{0,24},{8,16},{16,8},{24,0},{1,25},{9,17},{17,9},{25,1},{2,26},{10... | collective-permute-start | bytes 294920 | tf_op jit(solution)/shard_map/ppermute | solution.py:367
  10.8 14.4 %collective-permute-start.7 = (f32[56,8,128]{2,1,0:T(8,128)S(1)}, f32[56,8,128]{2,1,0:T(8,128)S(1)}, u32[]{:S(2)}, u32[]{:S(2)}) collective-permute-start(f32[56,8,128]{2,1,0:T(8,128)S(1)} %shard_map.32), channel_id=1, source_target_pairs={{0,4},{4,0},{1,5},{5,1},{2,6},{6,2},{3,7},{7,3},{8,12},{12,8},{9,1... | collective-permute-start | bytes 688136 | tf_op jit(solution)/shard_map/ppermute | solution.py:367
  10.8 3.7 %collective-permute-start.2 = (f32[16,128]{1,0:T(8,128)S(1)}, f32[16,128]{1,0:T(8,128)S(1)}, u32[]{:S(2)}, u32[]{:S(2)}) collective-permute-start(f32[16,128]{1,0:T(8,128)S(1)} %get-tuple-element.21), channel_id=1, source_target_pairs={{0,8},{8,0},{16,24},{24,16},{1,9},{9,1},{17,25},{25,17},{2,10},{10... | collective-permute-start | bytes 24584 | tf_op jit(solution)/shard_map/ppermute | solution.py:367
  12.3 4.5 %collective-permute-start.3 = (f32[16,128]{1,0:T(8,128)S(1)}, f32[16,128]{1,0:T(8,128)S(1)}, u32[]{:S(2)}, u32[]{:S(2)}) collective-permute-start(f32[16,128]{1,0:T(8,128)S(1)} %get-tuple-element.22), channel_id=1, source_target_pairs={{0,24},{8,16},{16,8},{24,0},{1,25},{9,17},{17,9},{25,1},{2,26},{10... | collective-permute-start | bytes 24584 | tf_op jit(solution)/shard_map/ppermute | solution.py:367
  16.9 1.2 %collective-permute-start.4 = (f32[2,8,128]{2,1,0:T(8,128)S(1)}, f32[2,8,128]{2,1,0:T(8,128)S(1)}, u32[]{:S(2)}, u32[]{:S(2)}) collective-permute-start(f32[2,8,128]{2,1,0:T(8,128)S(1)} %get-tuple-element.24), channel_id=1, source_target_pairs={{0,4},{4,0},{1,5},{5,1},{2,6},{6,2},{3,7},{7,3},{8,12},{12,8},{9,1... | collective-permute-start | bytes 24584 | tf_op jit(solution)/shard_map/ppermute | solution.py:367
  18.1 4.1 %collective-permute-start.5 = (f32[24,128]{1,0:T(8,128)S(1)}, f32[24,128]{1,0:T(8,128)S(1)}, u32[]{:S(2)}, u32[]{:S(2)}) collective-permute-start(f32[24,128]{1,0:T(8,128)S(1)} %get-tuple-element.25.own_a), channel_id=1, source_target_pairs={{0,1},{1,0},{2,3},{3,2},{4,5},{5,4},{6,7},{7,6},{8,9},{9,8},{10,11... | collective-permute-start | bytes 36872 | tf_op jit(solution)/shard_map/ppermute | solution.py:367
  19.7 5.5 %collective-permute-start.6 = (f32[24,128]{1,0:T(8,128)S(1)}, f32[24,128]{1,0:T(8,128)S(1)}, u32[]{:S(2)}, u32[]{:S(2)}) collective-permute-start(f32[24,128]{1,0:T(8,128)S(1)} %get-tuple-element.26.own_b), channel_id=1, source_target_pairs={{0,3},{1,2},{2,1},{3,0},{4,7},{5,6},{6,5},{7,4},{8,11},{9,10},{10,... | collective-permute-start | bytes 36872 | tf_op jit(solution)/shard_map/ppermute | solution.py:367
